TPU v7x, 128 devices: a whole 4x4x4 slice. The times are simulated.
128 devices in a mesh: seq: 16 (over z_hi, y, core), tensor: 8 (over z_lo, x).
Axes of the slice: x: 4, y: 4, z: 4 (z_hi: 2, z_lo: 2; z = z_hi * 2 + z_lo), core: 2. Of those that a mesh axis runs over, the one named last changes fastest.
Arguments:
- tokens: bfloat16 [11520, 1536], P('seq'), may hold values from -6 to 6
- norm_gain: float32 [1536], replicated, may hold values from 0.1 to 1.9
- w_qkv: bfloat16 [1536, 3, 1536], P(None, None, 'tensor'), may hold values from -8 to 8
- w_out: bfloat16 [1536, 1536], P('tensor'), may hold values from -0.15625 to 0.15625
- post_gain: float32 [1536], replicated, may hold values from 0.1 to 1.9
- w_up: bfloat16 [1536, 6144], P(None, 'tensor'), may hold values from -0.15625 to 0.15625
- w_down: bfloat16 [6144, 1536], P('tensor'), may hold values from -0.078125 to 0.078125
Outputs:
- layer_out: bfloat16 [11520, 1536], P('seq')
All inputs are finite; a program needn't handle non-finite values.
Results may differ from a plain program's by a relative error of at most 0.015.
Values may be sent and summed in bfloat16 or wider, within the bound.
A program may use at most 128 MiB of HBM per device.

v0:
```python
import functools

import jax
import jax.numpy as jnp
from jax import lax
from jax.experimental import pallas as pl
from jax.experimental.pallas import tpu as pltpu
from jax.sharding import PartitionSpec as P

HD = 48
PAD = 768
WIDE = 1024
MESH = pl.DeviceIdType.MESH
LOG2E = 1.4426950408889634
LIMIT = 2.0**90
FLOOR = 2.0**-20
FULL = pl.BlockSpec(memory_space=pltpu.VMEM)


def layer_norm(values, gain):
    mean = jnp.mean(values, axis=-1, keepdims=True)
    centred = values - mean
    var = jnp.mean(centred * centred, axis=-1, keepdims=True)
    return centred * lax.rsqrt(var + 1e-05) * gain


def sweep(rows, blocks, queries, keys, vals, acc, probs, unroll, stage):
    chunks = queries.shape[1] // WIDE
    total = blocks * chunks

    def place(i):
        return i // chunks, pl.ds(pl.multiple_of(lax.rem(i, chunks) * WIDE, WIDE), WIDE)

    def scores(i, slot):
        b, cols = place(i)
        s = jnp.dot(keys[b, 0:rows], queries[:, cols], preferred_element_type=jnp.float32)
        probs[slot, 0:rows, :] = jnp.exp2(s).astype(jnp.bfloat16)

    def product(i, slot):
        b, cols = place(i)
        acc[:, cols] += jnp.dot(vals[b], probs[slot], preferred_element_type=jnp.float32)

    scores(0, 0)

    def body(j, _):
        for k in range(total // unroll):

            @pl.when(j == k)
            def _(k=k):
                stage(k)

        for u in range(unroll):
            i = unroll * j + u
            ahead = i + 1 if u < unroll - 1 else jnp.minimum(i + 1, total - 1)
            scores(ahead, (u + 1) % 2)
            product(i, u % 2)
        return 0

    lax.fori_loop(0, total // unroll, body, 0)


ORDER = (0, 1, 3, 2)


def load_block(rows, kv, b, keys, vals):
    lane = lax.broadcasted_iota(jnp.int32, (16, PAD), 1)
    sub = lax.broadcasted_iota(jnp.int32, (16, PAD), 0)
    count = ((sub == 0) & (lane < rows)).astype(jnp.float32).astype(jnp.bfloat16)
    shift = (sub == 0).astype(jnp.float32).astype(jnp.bfloat16)
    zeros = jnp.zeros((64, PAD), jnp.bfloat16)
    keys[b] = jnp.concatenate([kv[0], shift, zeros], axis=0).T
    vals[b, 0:HD] = kv[1]
    vals[b, HD : HD + 16] = count


def attend_kernel(rows, qkv, w_ref, acc, land, kvx, w_all, queries, keys, vals, probs, w_own, send, recv, local):
    width = queries.shape[1]
    seq, me = lax.axis_index("seq"), lax.axis_index("tensor")
    z, y, core = seq // 8, lax.rem(seq // 2, 4), lax.rem(seq, 2)
    links = Links(send, recv)

    def on_seq(dz, dy, dc):
        return ((lax.rem(z + dz, 2) * 4 + lax.rem(y + dy, 4)) * 2 + lax.rem(core + dc, 2), me)

    barrier = pltpu.get_barrier_semaphore()
    peers = [on_seq(0, d, 0) for d in (1, 2, 3)] + [on_seq(0, 0, 1), on_seq(1, 0, 0)]
    peers += [(seq, links.slot(1, 0)), (seq, links.slot(0, 1)), (seq, links.slot(0, 3))]
    for peer in peers:
        pl.semaphore_signal(barrier, inc=1, device_id=peer, device_id_type=MESH)
    pl.semaphore_wait(barrier, 8)

    by_y = {}
    for d in (2, 1, 3):
        by_y[d] = links.start(lambda d=d: (qkv.at[:, lax.rem(y + d, 4)], land.at[d], on_seq(0, d, 0)))
    to_core, to_far, far_core = {}, {}, {}
    to_core[0] = links.start(lambda: (qkv.at[1:3, y], kvx.at[0, 0], on_seq(0, 0, 1)))
    to_far[0] = links.start(lambda: (qkv.at[1:3, y], kvx.at[1, 0], on_seq(1, 0, 0)))

    fetch = pltpu.make_async_copy(w_ref, w_own, local.at[0])
    fetch.start()
    land[0] = qkv[:, y]
    load_block(rows, land.at[0, 1:3], 0, keys, vals)
    fetch.wait()
    keep = pltpu.make_async_copy(w_own, w_all.at[me], local.at[1])
    keep.start()
    w_cols = w_own.shape[2] // 2

    def tensor_at(dz, dx):
        return (seq, links.slot(dz, dx))

    def own_w(dz, dx):
        return links.start(lambda: (w_own.at[core], w_all.at[me, core], tensor_at(dz, dx)))

    def pass_w(slot, lo, hi, dz, dx):
        def ends():
            ref = w_all.at[links.slot(*slot), core, :, lo * w_cols : hi * w_cols]
            return ref, ref, tensor_at(dz, dx)

        return links.start(ends)

    def swap_w(slot):
        def ends():
            ref = w_all.at[links.slot(*slot), core]
            return ref, ref, on_seq(0, 0, 1)

        return links.start(ends)

    wz, wup, wdown = own_w(1, 0), own_w(0, 1), own_w(0, 3)

    acc[...] = jnp.zeros_like(acc)
    probs[:, rows:PAD, :] = jnp.zeros((2, PAD - rows, WIDE), jnp.bfloat16)
    queries[HD:128, :] = jnp.zeros((128 - HD, width), jnp.bfloat16)
    queries[0:HD, 0:PAD] = land[0, 0]
    for i in (1, 2, 3):
        d = ORDER[i]
        by_y[d].wait_recv()
        to_core[d] = links.start(lambda d=d: (land.at[d, 1:3], kvx.at[0, d], on_seq(0, 0, 1)))
        to_far[d] = links.start(lambda d=d: (land.at[d, 1:3], kvx.at[1, d], on_seq(1, 0, 0)))
        load_block(rows, land.at[d, 1:3], i, keys, vals)
        queries[0:HD, d * PAD : (d + 1) * PAD] = land[d, 0]

    for c in range(width // WIDE):
        cols = slice(c * WIDE, (c + 1) * WIDE)
        s = jnp.dot(keys[0, 0:rows], queries[:, cols], preferred_element_type=jnp.float32)
        top = jnp.max(s.reshape(rows // 8, 8, WIDE), axis=0)
        top = jnp.max(top, axis=0, keepdims=True)
        first = lax.broadcasted_iota(jnp.int32, (16, WIDE), 0) == 0
        shift = jnp.where(first, jnp.broadcast_to(-top, (16, WIDE)), 0.0)
        queries[HD : HD + 16, cols] = shift.astype(jnp.bfloat16)

    more = {}

    def take(block):
        group, d = block // 4, ORDER[block % 4]
        if group == 1:
            to_core[d].wait_recv()
        elif group == 2:
            to_far[d].wait_recv()
            far_core[d] = links.start(lambda d=d: (kvx.at[1, d], kvx.at[2, d], on_seq(0, 0, 1)))
        elif group == 3:
            far_core[d].wait_recv()
        load_block(rows, kvx.at[group - 1, d], block, keys, vals)

    others = [(0, 1), (0, 2), (0, 3), (1, 0), (1, 1), (1, 2), (1, 3)]

    def stage(j):
        for block in (2 * j + 1, 2 * j + 2):
            if 4 <= block < 16:
                take(block)
        if j == 1:
            wz.wait_recv()
            more["zup"] = pass_w((1, 0), 0, 2, 0, 1)
            more["zdown"] = pass_w((1, 0), 0, 2, 0, 3)
            wup.wait_recv()
            more["r0"] = pass_w((0, 3), 0, 1, 0, 1)
            wdown.wait_recv()
            more["r1"] = pass_w((0, 1), 1, 2, 0, 3)
        if j == 3:
            more["zup"].wait_recv()
            more["q0"] = pass_w((1, 3), 0, 1, 0, 1)
            more["zdown"].wait_recv()
            more["q1"] = pass_w((1, 1), 1, 2, 0, 3)
        if j == 6:
            for name in ("r0", "r1", "q0", "q1"):
                more[name].wait_recv()
            for dz, dx in others:
                more[dz, dx] = swap_w((dz, dx))

    sweep(rows, 16, queries, keys, vals, acc, probs, 6, stage)
    keep.wait()
    for pair in others:
        more[pair].wait_recv()
    links.drain()


def settle_kernel(rows, acc_in, land, kvx, o_ref, queries, keys, vals, probs, acc):
    width = acc_in.shape[1]
    total = acc_in[HD : HD + 1, :]
    fits = jnp.where((total < LIMIT) & (total > FLOOR), 0.0, 1.0)
    again = jnp.max(fits) > 0.5

    def write(sums):
        for d in range(4):
            cols = slice(d * PAD, (d + 1) * PAD)
            o_ref[d] = (sums[0:HD, cols] / sums[HD : HD + 1, cols]).astype(jnp.bfloat16)

    @pl.when(jnp.logical_not(again))
    def _():
        write(acc_in)

    @pl.when(again)
    def _():
        queries[HD:128, :] = jnp.zeros((128 - HD, width), jnp.bfloat16)
        for d in range(4):
            queries[0:HD, d * PAD : (d + 1) * PAD] = land[d, 0]
        probs[rows:PAD, :] = jnp.zeros((PAD - rows, 256), jnp.bfloat16)
        acc[...] = jnp.zeros_like(acc)

        def fill(d, _):
            load_block(rows, land.at[d, 1:3], d, keys, vals)
            for g in range(3):
                load_block(rows, kvx.at[g, d], 4 * g + 4 + d, keys, vals)
            return 0

        lax.fori_loop(0, 4, fill, 0)

        def chunk(c, _):
            cols = pl.ds(pl.multiple_of(c * 256, 256), 256)

            def block(b, carry):
                peak, sums = carry
                s = jnp.dot(keys[b, 0:rows], queries[:, cols], preferred_element_type=jnp.float32)
                fresh = jnp.maximum(peak, jnp.max(s, axis=0, keepdims=True))
                probs[0:rows, :] = jnp.exp2(s - fresh).astype(jnp.bfloat16)
                part = jnp.dot(vals[b], probs[...], preferred_element_type=jnp.float32)
                return fresh, sums * jnp.exp2(peak - fresh) + part

            start = (jnp.full((1, 256), -1e30, jnp.float32), jnp.zeros((HD + 16, 256), jnp.float32))
            _, sums = lax.fori_loop(0, 16, block, start)
            acc[:, cols] = sums
            return 0

        lax.fori_loop(0, width // 256, chunk, 0)
        write(acc)


def attention(rows, qkv, w_out):
    width = 4 * PAD
    bf16 = jnp.bfloat16
    half, cols = w_out.shape[0] // 2, w_out.shape[1]
    n = 48
    tables = [
        pltpu.VMEM((128, width), bf16),
        pltpu.VMEM((16, PAD, 128), bf16),
        pltpu.VMEM((16, HD + 16, PAD), bf16),
    ]
    anywhere = pl.BlockSpec(memory_space=pl.ANY)
    acc, land, kvx, w_all = pl.pallas_call(
        functools.partial(attend_kernel, rows),
        out_shape=(
            jax.ShapeDtypeStruct((HD + 16, width), jnp.float32),
            jax.ShapeDtypeStruct((4, 3, HD, PAD), bf16),
            jax.ShapeDtypeStruct((3, 4, 2, HD, PAD), bf16),
            jax.ShapeDtypeStruct((8, 2, half, cols), bf16),
        ),
        in_specs=[FULL, anywhere],
        out_specs=(FULL, FULL, FULL, anywhere),
        scratch_shapes=tables
        + [
            pltpu.VMEM((2, PAD, WIDE), bf16),
            pltpu.VMEM((2, half, cols), bf16),
            pltpu.SemaphoreType.DMA((n,)),
            pltpu.SemaphoreType.DMA((n,)),
            pltpu.SemaphoreType.DMA((2,)),
        ],
        compiler_params=pltpu.CompilerParams(collective_id=0, has_side_effects=True, vmem_limit_bytes=48 * 2**20),
        name="attend",
    )(qkv, w_out.reshape(2, half, cols))
    o = pl.pallas_call(
        functools.partial(settle_kernel, rows),
        out_shape=jax.ShapeDtypeStruct((4, HD, PAD), bf16),
        in_specs=[FULL] * 3,
        out_specs=FULL,
        scratch_shapes=tables + [pltpu.VMEM((PAD, 256), bf16), pltpu.VMEM((HD + 16, width), jnp.float32)],
        compiler_params=pltpu.CompilerParams(vmem_limit_bytes=40 * 2**20),
        name="settle",
    )(acc, land, kvx)
    return o, w_all.reshape(16 * half, cols)


class Links:
    def __init__(self, send, recv):
        me = lax.axis_index("tensor")
        self.seq = lax.axis_index("seq")
        self.z, self.x = me // 4, lax.rem(me, 4)
        self.me = me
        self.send, self.recv = send, recv
        self.count = 0
        self.open = []

    def slot(self, dz, dx):
        z = lax.rem(self.z + dz, 2)
        return z * 4 + lax.rem(self.x + dx, 4)

    def barrier(self, more=0):
        sem = pltpu.get_barrier_semaphore()
        for dz, dx in ((1, 0), (0, 1), (0, 3)):
            pl.semaphore_signal(sem, inc=1, device_id=(self.seq, self.slot(dz, dx)), device_id_type=MESH)
        pl.semaphore_wait(sem, 3 + more)

    def put(self, src, dst, dz, dx):
        device = (self.seq, self.slot(dz, dx))
        return self.start(lambda: (src, dst, device))

    def start(self, ends):
        copy = Copy(self, self.count, ends)
        self.count += 1
        self.open.append(copy)
        copy.make().start()
        return copy

    def drain(self):
        for copy in self.open:
            copy.make().wait_send()
        self.open = []


class Copy:
    def __init__(self, links, index, ends):
        self.links, self.index, self.ends = links, index, ends

    def make(self):
        src, dst, device = self.ends()
        return pltpu.make_async_remote_copy(
            src_ref=src,
            dst_ref=dst,
            send_sem=self.links.send.at[self.index],
            recv_sem=self.links.recv.at[self.index],
            device_id=device,
            device_id_type=MESH,
        )

    def wait_recv(self):
        self.make().wait_recv()


def gather_tensor(links, piece):
    s = links.slot
    put = links.put

    def pass_on(slot, lo, hi, dz, dx):
        ref = piece(slot, lo, hi)
        return put(ref, ref, dz, dx)

    me = s(0, 0)
    a_z = pass_on(me, 0, 2, 1, 0)
    b_up = pass_on(me, 2, 4, 0, 1)
    b_down = pass_on(me, 2, 4, 0, 3)
    b_z = pass_on(me, 2, 4, 1, 0)
    a_up = pass_on(me, 0, 2, 0, 1)
    a_down = pass_on(me, 0, 2, 0, 3)
    b_up.wait_recv()
    r2 = pass_on(s(0, 3), 2, 3, 0, 1)
    bz_lo = pass_on(s(0, 3), 2, 4, 1, 0)
    b_down.wait_recv()
    r3 = pass_on(s(0, 1), 3, 4, 0, 3)
    bz_hi = pass_on(s(0, 1), 2, 4, 1, 0)
    a_z.wait_recv()
    az_up = pass_on(s(1, 0), 0, 2, 0, 1)
    az_down = pass_on(s(1, 0), 0, 2, 0, 3)
    a_up.wait_recv()
    r0 = pass_on(s(0, 3), 0, 1, 0, 1)
    a_down.wait_recv()
    r1 = pass_on(s(0, 1), 1, 2, 0, 3)
    r2.wait_recv()
    bz_2 = pass_on(s(0, 2), 2, 3, 1, 0)
    r3.wait_recv()
    bz_3 = pass_on(s(0, 2), 3, 4, 1, 0)
    az_up.wait_recv()
    q0 = pass_on(s(1, 3), 0, 1, 0, 1)
    az_down.wait_recv()
    q1 = pass_on(s(1, 1), 1, 2, 0, 3)
    for copy in (b_z, bz_lo, bz_hi, r0, r1, bz_2, bz_3, q0, q1):
        copy.wait_recv()
    links.drain()


GATHER_COPIES = 18


def gather_heads_kernel(o_ref, out_ref, send, recv):
    links = Links(send, recv)
    seq = links.seq
    y = lax.rem(seq // 2, 4)

    def at_y(dy):
        return ((seq // 8 * 4 + lax.rem(y + dy, 4)) * 2 + lax.rem(seq, 2), links.me)

    sem = pltpu.get_barrier_semaphore()
    for d in (1, 2, 3):
        pl.semaphore_signal(sem, inc=1, device_id=at_y(d), device_id_type=MESH)
    links.barrier(3)
    back = [links.start(lambda d=d: (o_ref.at[d], out_ref.at[links.me, y], at_y(4 - d))) for d in (2, 1, 3)]
    out_ref[links.me, y] = o_ref[0]
    for copy in back:
        copy.wait_recv()
    gather_tensor(links, lambda slot, lo, hi: out_ref.at[slot, lo:hi])


def gather_heads(o):
    copies = GATHER_COPIES + 3
    return pl.pallas_call(
        gather_heads_kernel,
        out_shape=jax.ShapeDtypeStruct((8,) + o.shape, o.dtype),
        in_specs=[FULL],
        out_specs=FULL,
        scratch_shapes=[pltpu.SemaphoreType.DMA((copies,)), pltpu.SemaphoreType.DMA((copies,))],
        compiler_params=pltpu.CompilerParams(collective_id=1, has_side_effects=True, vmem_limit_bytes=32 * 2**20),
        name="gather_heads",
    )(o)


def reduce_tensor(links, term, stage, rows, cols):
    quarter = cols // 4
    s = links.slot
    put = links.put

    def q(slot, lo, hi):
        return term.at[slot, :, lo * quarter : hi * quarter]

    def val(slot, lo, hi):
        return term[slot, :, lo * quarter : hi * quarter].astype(jnp.float32)

    def land(i, n):
        return stage.at[i, :, 0 : n * quarter]

    def got(i, lo, hi):
        return stage[i, :, lo * quarter : hi * quarter].astype(jnp.float32)

    def add_into(slot, lo, hi, *parts):
        total = val(slot, lo, hi)
        for part in parts:
            total = total + part
        term[slot, :, lo * quarter : hi * quarter] = total.astype(jnp.bfloat16)

    zb = {}
    for i, dx in enumerate((2, 1, 3, 0)):
        zb[dx] = put(q(s(1, dx), 2, 4), land(i, 2), 1, 0)
    fa = {}
    for j, dz in enumerate((1, 0)):
        fa[dz, 0] = put(q(s(dz, 2), 0, 1), land(4 + j, 1), 0, 3)
        fa[dz, 1] = put(q(s(dz, 2), 1, 2), land(6 + j, 1), 0, 1)
    near = {}
    for j, dz in enumerate((1, 0)):
        fa[dz, 0].wait_recv()
        add_into(s(dz, 3), 0, 1, got(4 + j, 0, 1))
        near[dz, 3] = put(q(s(dz, 3), 0, 2), land(8 + j, 2), 0, 3)
        fa[dz, 1].wait_recv()
        add_into(s(dz, 1), 1, 2, got(6 + j, 0, 1))
        near[dz, 1] = put(q(s(dz, 1), 0, 2), land(10 + j, 2), 0, 1)
    zb[2].wait_recv()
    add_into(s(0, 2), 2, 4, got(0, 0, 2))
    fb0 = put(q(s(0, 2), 2, 3), land(12, 1), 0, 3)
    fb1 = put(q(s(0, 2), 3, 4), land(13, 1), 0, 1)
    zb[1].wait_recv()
    zb[3].wait_recv()
    near[1, 3].wait_recv()
    near[1, 1].wait_recv()
    add_into(s(1, 0), 0, 2, got(8, 0, 2), got(10, 0, 2))
    za = put(q(s(1, 0), 0, 2), land(14, 2), 1, 0)
    fb0.wait_recv()
    add_into(s(0, 3), 2, 3, got(2, 0, 1), got(12, 0, 1))
    add_into(s(0, 3), 3, 4, got(2, 1, 2))
    nb3 = put(q(s(0, 3), 2, 4), land(15, 2), 0, 3)
    fb1.wait_recv()
    add_into(s(0, 1), 3, 4, got(1, 1, 2), got(13, 0, 1))
    add_into(s(0, 1), 2, 3, got(1, 0, 1))
    nb1 = put(q(s(0, 1), 2, 4), land(16, 2), 0, 1)
    near[0, 3].wait_recv()
    near[0, 1].wait_recv()
    za.wait_recv()
    first = val(s(0, 0), 0, 2) + got(9, 0, 2) + got(11, 0, 2) + got(14, 0, 2)
    zb[0].wait_recv()
    nb3.wait_recv()
    nb1.wait_recv()
    second = val(s(0, 0), 2, 4) + got(3, 0, 2) + got(15, 0, 2) + got(16, 0, 2)
    links.drain()
    return first, second


def finish_kernel(term_in, mixed_ref, out_ref, term, stage, send, recv):
    rows, cols = mixed_ref.shape
    quarter = cols // 4
    links = Links(send, recv)
    links.barrier()
    term[...] = term_in[...]
    first, second = reduce_tensor(links, term, stage, rows, cols)
    out_ref[links.me, :, 0 : 2 * quarter] = (mixed_ref[:, 0 : 2 * quarter] + first).astype(jnp.bfloat16)
    out_ref[links.me, :, 2 * quarter :] = (mixed_ref[:, 2 * quarter :] + second).astype(jnp.bfloat16)
    gather_tensor(links, lambda slot, lo, hi: out_ref.at[slot, :, lo * quarter : hi * quarter])


def finish(term, mixed):
    parts, rows, cols = term.shape
    copies = 40
    return pl.pallas_call(
        finish_kernel,
        out_shape=jax.ShapeDtypeStruct(term.shape, jnp.bfloat16),
        in_specs=[FULL, FULL],
        out_specs=FULL,
        scratch_shapes=[
            pltpu.VMEM(term.shape, jnp.bfloat16),
            pltpu.VMEM((17, rows, cols // 2), jnp.bfloat16),
            pltpu.SemaphoreType.DMA((copies,)),
            pltpu.SemaphoreType.DMA((copies,)),
        ],
        compiler_params=pltpu.CompilerParams(collective_id=2, has_side_effects=True, vmem_limit_bytes=40 * 2**20),
        name="finish",
    )(term, mixed)


def per_device(tokens, norm_gain, w_qkv, w_out, post_gain, w_up, w_down):
    rows, width = tokens.shape
    heads = w_qkv.shape[2] // HD
    t = lax.axis_index("tensor")
    base = tokens.astype(jnp.float32)
    normed = layer_norm(base, norm_gain).astype(jnp.bfloat16)
    qkv = lax.dot_general(w_qkv, normed, (((0,), (1,)), ((), ())), preferred_element_type=jnp.float32)
    factor = jnp.array([LOG2E / HD**0.5, 1.0, 1.0], jnp.float32)[:, None, None]
    qkv = (qkv * factor).astype(jnp.bfloat16)
    qkv = jnp.pad(qkv, ((0, 0), (0, 0), (0, PAD - rows))).reshape(3, heads, HD, PAD)

    o, w_out_all = attention(rows, qkv, w_out)
    every = gather_heads(o).reshape(8 * heads * HD, PAD)
    padded = jnp.pad(base, ((0, PAD - rows), (0, 0)))
    mixed = padded + lax.dot_general(
        every, w_out_all, (((0,), (0,)), ((), ())), preferred_element_type=jnp.float32
    )
    post = layer_norm(mixed, post_gain).astype(jnp.bfloat16)
    hidden = jax.nn.gelu(
        jnp.dot(post, w_up, preferred_element_type=jnp.float32), approximate=True
    ).astype(jnp.bfloat16)
    term = jnp.dot(hidden, w_down, preferred_element_type=jnp.float32).astype(jnp.bfloat16)
    share = PAD // 8
    mine = lax.dynamic_slice_in_dim(mixed, t * share, share, 0)
    out = finish(term.reshape(8, share, width), mine)
    return out.reshape(PAD, width)[:rows]


def solution(mesh):
    placed = (
        P("seq", None),
        P(),
        P(None, None, "tensor"),
        P("tensor", None),
        P(),
        P(None, "tensor"),
        P("tensor", None),
    )
    return jax.shard_map(
        per_device, mesh=mesh, in_specs=placed, out_specs=P("seq", None), check_vma=False
    )
```

profile of v0, /device:TPU:0, one launch (start us, length us, event | category | flops | bytes accessed | tf_op | source)
XLA Modules:
  0.0 255.6 jit_solution(15726790228437351665)
XLA Ops:
  0.0 0.0 copy-start
  0.0 0.0 copy-start.4
  0.0 0.0 copy-start.7
  0.0 0.0 copy-start.8
  0.0 2.1 convert_reduce_fusion
  2.2 0.3 copy-done.4
  2.4 0.7 multiply_reduce_fusion.1
  3.2 0.0 copy-done.7
  3.2 0.0 copy-done.8
  3.2 0.0 copy-start.6
  3.2 1.7 fusion.12
  4.9 0.0 copy-start.2
  5.0 0.0 copy-done.6
  5.0 0.2 fusion.16
  5.2 0.1 pad.9
  5.3 0.8 copy-done.2
  6.0 55.4 %attend.1 = (f32[64,3072]{1,0:T(8,128)S(1)}, bf16[4,3,48,768]{3,2,1,0:T(8,128)(2,1)S(1)}, bf16[3,4,2,48,768]{4,3,2,1,0:T(8,128)(2,1)S(1)}, bf16[8,2,96,1536]{3,2,1,0:T(8,128)(2,1)}) custom-call(bf16[3,4,48,768]{3,2,1,0:T(8,128)(2,1)S(1)} %bitcast.17, bf16[2,96,1536]{2,1,0:T(8,128)(2,1)S(1)} %bitcast.19), custom_call_target="tpu_custom_call" | custom-call | tf_op jit(solution)/shard_map/attend/pallas_call | solution.py:258
  61.4 0.4 settle.1.o_ref
  61.8 136.5 %gather_heads.1 = bf16[8,4,48,768]{3,2,1,0:T(8,128)(2,1)S(1)} custom-call(bf16[4,48,768]{2,1,0:T(8,128)(2,1)S(1)} %settle.1.o_ref), custom_call_target="tpu_custom_call" | custom-call | tf_op jit(solution)/shard_map/gather_heads/pallas_call | solution.py:412
  198.3 0.0 copy-start.5
  198.3 0.6 convert_element_type.25
  198.9 1.7 copy-done.5
  200.6 3.9 %fusion.21 = (f32[768]{0:T(1024)S(1)}, f32[768,1536]{1,0:T(8,128)S(1)}) fusion(bf16[1536,768]{1,0:T(8,128)(2,1)S(1)} %bitcast.15, bf16[1536,1536]{1,0:T(8,128)(2,1)S(1)} %bitcast.20, f32[720,1536]{1,0:T(8,128)S(1)} %convert_element_type.25), kind=kOutput, calls=%fused_computation.35 | convolution fusion | flops 3626237184 | bytes 16223232 | tf_op jit(solution)/shard_map/dot_general | solution.py:536
  204.5 0.0 copy-start.3
  204.6 0.0 copy-start.9
  204.6 0.6 multiply_reduce_fusion
  205.2 1.5 copy-done.3
  206.7 0.0 copy-done
  206.7 0.0 copy-done.9
  206.7 9.3 %convolution_convert_fusion = bf16[768,1536]{1,0:T(8,128)(2,1)} fusion(bf16[768,1536]{1,0:T(8,128)(2,1)S(1)} %copy-done, bf16[1536,768]{1,0:T(8,128)(2,1)} %param.13, f32[768,1536]{1,0:T(8,128)} %copy-done.3, f32[1536]{0:T(1024)S(1)} %copy-done.9, f32[768]{0:T(1024)S(1)} %add_rsqrt_fusion, f32[768]{0:T(1024)S(1)} %broadcast_multiply_fusion), kind=kOutput, calls=%fused_computation.6 | convolution fusion | flops 3635085312 | bytes 11808768 | tf_op jit(solution)/shard_map/dot_general | solution.py:543
  216.0 1.1 constant_dynamic-slice_fusion.mixed_ref
  217.1 0.0 copy-start.1
  217.1 1.7 copy-done.1
  218.8 35.3 %finish.1 = bf16[8,96,1536]{2,1,0:T(8,128)(2,1)S(1)} custom-call(bf16[8,96,1536]{2,1,0:T(8,128)(2,1)S(1)} %bitcast.18, f32[96,1536]{1,0:T(8,128)S(1)} %constant_dynamic-slice_fusion.mixed_ref), custom_call_target="tpu_custom_call" | custom-call | tf_op jit(solution)/shard_map/finish/pallas_call | solution.py:506
  254.1 1.5 slice.4
  (4 shorter events, 0.0 us)
Async XLA Ops:
  0.0 206.7 %copy-start = (bf16[768,1536]{1,0:T(8,128)(2,1)S(1)}, bf16[768,1536]{1,0:T(8,128)(2,1)}, u32[]{:S(2)}) copy-start(bf16[768,1536]{1,0:T(8,128)(2,1)} %param.14) | copy-start | bytes 7077892
  0.0 2.4 copy-start.4
  0.0 3.2 %copy-start.7 = (bf16[1536,3,192]{0,2,1:T(8,128)(2,1)S(1)}, bf16[1536,3,192]{0,2,1:T(8,128)(2,1)}, u32[]{:S(2)}) copy-start(bf16[1536,3,192]{0,2,1:T(8,128)(2,1)} %param.10) | copy-start | bytes 5308420
  0.0 3.2 %copy-start.8 = (f32[1536]{0:T(1024)S(1)}, f32[1536]{0:T(1024)}, u32[]{:S(2)}) copy-start(f32[1536]{0:T(1024)} %param.9) | copy-start | bytes 18436
  3.2 1.8 copy-start.6
  4.9 1.1 copy-start.2
  198.3 2.3 copy-start.5
  204.5 2.1 copy-start.3
  204.6 2.1 copy-start.9
  217.1 1.7 copy-start.1
where the time goes:
time: 256 us
  Pallas kernels  228 us (89%)
  matrix products  15 us (6%)
  local copies, waits for them, and re-layouts  8.64 us (3%)
  other arithmetic  4.25 us (2%)
    pallas_call x1, Pallas kernels, gather_heads(): pl.pallas_call(gather_heads_kernel, out_shape=jax.ShapeDtypeStruct((8,) +...  136 us
    pallas_call x1, Pallas kernels, attention(): pl.pallas_call(functools.partial(attend_kernel, rows), out_shape=(jax.Sha...  55.4 us
    pallas_call x1, Pallas kernels, finish(): pl.pallas_call(finish_kernel, out_shape=jax.ShapeDtypeStruct(term.shape,...  35.3 us
    dot_general x1, matrix products, per_device(): jnp.dot(hidden, w_down, preferred_element_type=jnp.float32)  9.34 us
    unnamed x20, local copies, waits for them, and re-layouts  5.96 us

commit v1 on v0

--- a/solution.py
+++ b/solution.py
@@ -344,7 +344,7 @@
         self.make().wait_recv()
 
 
-def gather_tensor(links, piece):
+def gather_tensor(links, piece, ready=lambda dz, dx: None):
     s = links.slot
     put = links.put
 
@@ -359,6 +359,7 @@
     b_z = pass_on(me, 2, 4, 1, 0)
     a_up = pass_on(me, 0, 2, 0, 1)
     a_down = pass_on(me, 0, 2, 0, 3)
+    ready(0, 0)
     b_up.wait_recv()
     r2 = pass_on(s(0, 3), 2, 3, 0, 1)
     bz_lo = pass_on(s(0, 3), 2, 4, 1, 0)
@@ -372,55 +373,35 @@
     r0 = pass_on(s(0, 3), 0, 1, 0, 1)
     a_down.wait_recv()
     r1 = pass_on(s(0, 1), 1, 2, 0, 3)
+    ready(0, 3)
     r2.wait_recv()
     bz_2 = pass_on(s(0, 2), 2, 3, 1, 0)
     r3.wait_recv()
     bz_3 = pass_on(s(0, 2), 3, 4, 1, 0)
+    ready(0, 1)
     az_up.wait_recv()
     q0 = pass_on(s(1, 3), 0, 1, 0, 1)
     az_down.wait_recv()
     q1 = pass_on(s(1, 1), 1, 2, 0, 3)
-    for copy in (b_z, bz_lo, bz_hi, r0, r1, bz_2, bz_3, q0, q1):
+    b_z.wait_recv()
+    ready(1, 0)
+    r0.wait_recv()
+    r1.wait_recv()
+    ready(0, 2)
+    bz_lo.wait_recv()
+    ready(1, 3)
+    bz_hi.wait_recv()
+    ready(1, 1)
+    for copy in (bz_2, bz_3, q0, q1):
         copy.wait_recv()
+    ready(1, 2)
     links.drain()
 
 
 GATHER_COPIES = 18
 
 
-def gather_heads_kernel(o_ref, out_ref, send, recv):
-    links = Links(send, recv)
-    seq = links.seq
-    y = lax.rem(seq // 2, 4)
-
-    def at_y(dy):
-        return ((seq // 8 * 4 + lax.rem(y + dy, 4)) * 2 + lax.rem(seq, 2), links.me)
-
-    sem = pltpu.get_barrier_semaphore()
-    for d in (1, 2, 3):
-        pl.semaphore_signal(sem, inc=1, device_id=at_y(d), device_id_type=MESH)
-    links.barrier(3)
-    back = [links.start(lambda d=d: (o_ref.at[d], out_ref.at[links.me, y], at_y(4 - d))) for d in (2, 1, 3)]
-    out_ref[links.me, y] = o_ref[0]
-    for copy in back:
-        copy.wait_recv()
-    gather_tensor(links, lambda slot, lo, hi: out_ref.at[slot, lo:hi])
-
-
-def gather_heads(o):
-    copies = GATHER_COPIES + 3
-    return pl.pallas_call(
-        gather_heads_kernel,
-        out_shape=jax.ShapeDtypeStruct((8,) + o.shape, o.dtype),
-        in_specs=[FULL],
-        out_specs=FULL,
-        scratch_shapes=[pltpu.SemaphoreType.DMA((copies,)), pltpu.SemaphoreType.DMA((copies,))],
-        compiler_params=pltpu.CompilerParams(collective_id=1, has_side_effects=True, vmem_limit_bytes=32 * 2**20),
-        name="gather_heads",
-    )(o)
-
-
-def reduce_tensor(links, term, stage, rows, cols):
+def reduce_tensor(links, term, stage, rows, cols, make):
     quarter = cols // 4
     s = links.slot
     put = links.put
@@ -443,25 +424,39 @@
             total = total + part
         term[slot, :, lo * quarter : hi * quarter] = total.astype(jnp.bfloat16)
 
-    zb = {}
-    for i, dx in enumerate((2, 1, 3, 0)):
+    zb, fa, near = {}, {}, {}
+
+    def cross(i, dx):
         zb[dx] = put(q(s(1, dx), 2, 4), land(i, 2), 1, 0)
-    fa = {}
-    for j, dz in enumerate((1, 0)):
+
+    def far(j, dz):
         fa[dz, 0] = put(q(s(dz, 2), 0, 1), land(4 + j, 1), 0, 3)
         fa[dz, 1] = put(q(s(dz, 2), 1, 2), land(6 + j, 1), 0, 1)
-    near = {}
-    for j, dz in enumerate((1, 0)):
+
+    def relay(j, dz):
         fa[dz, 0].wait_recv()
         add_into(s(dz, 3), 0, 1, got(4 + j, 0, 1))
         near[dz, 3] = put(q(s(dz, 3), 0, 2), land(8 + j, 2), 0, 3)
         fa[dz, 1].wait_recv()
         add_into(s(dz, 1), 1, 2, got(6 + j, 0, 1))
         near[dz, 1] = put(q(s(dz, 1), 0, 2), land(10 + j, 2), 0, 1)
+
+    make((1, 2), (1, 0))
+    cross(0, 2)
+    far(0, 1)
+    far(1, 0)
+    make((1, 1), (0, 2))
+    cross(1, 1)
+    cross(2, 3)
+    relay(0, 1)
+    make((0, 1), (0, 2))
+    relay(1, 0)
     zb[2].wait_recv()
     add_into(s(0, 2), 2, 4, got(0, 0, 2))
     fb0 = put(q(s(0, 2), 2, 3), land(12, 1), 0, 3)
     fb1 = put(q(s(0, 2), 3, 4), land(13, 1), 0, 1)
+    make((1, 0), (1, 0))
+    cross(3, 0)
     zb[1].wait_recv()
     zb[3].wait_recv()
     near[1, 3].wait_recv()
@@ -488,41 +483,108 @@
     return first, second
 
 
-def finish_kernel(term_in, mixed_ref, out_ref, term, stage, send, recv):
-    rows, cols = mixed_ref.shape
-    quarter = cols // 4
+def tail_kernel(
+    o_ref, w_out, tokens, gain, w_up, w_down, out_ref, every, mixed, post, term, stage, wo, tok, wu, wd, send, recv, local
+):
     links = Links(send, recv)
-    links.barrier()
-    term[...] = term_in[...]
-    first, second = reduce_tensor(links, term, stage, rows, cols)
-    out_ref[links.me, :, 0 : 2 * quarter] = (mixed_ref[:, 0 : 2 * quarter] + first).astype(jnp.bfloat16)
-    out_ref[links.me, :, 2 * quarter :] = (mixed_ref[:, 2 * quarter :] + second).astype(jnp.bfloat16)
+    seq, me = links.seq, links.me
+    y = lax.rem(seq // 2, 4)
+    share, width = out_ref.shape[1], out_ref.shape[2]
+    quarter = width // 4
+    rows = tok.shape[0]
+    loads = [
+        pltpu.make_async_copy(src, dst, local.at[i])
+        for i, (src, dst) in enumerate(((tokens, tok), (w_out, wo), (w_up, wu), (w_down, wd)))
+    ]
+    for load in loads:
+        load.start()
+
+    def at_y(dy):
+        return ((seq // 8 * 4 + lax.rem(y + dy, 4)) * 2 + lax.rem(seq, 2), me)
+
+    sem = pltpu.get_barrier_semaphore()
+    for d in (1, 2, 3):
+        pl.semaphore_signal(sem, inc=1, device_id=at_y(d), device_id_type=MESH)
+    links.barrier(3)
+    back = [links.start(lambda d=d: (o_ref.at[d], every.at[me, y], at_y(4 - d))) for d in (2, 1, 3)]
+    every[me, y] = o_ref[0]
+    loads[0].wait()
+    mixed[0:rows, :] = tok[...].astype(jnp.float32)
+    mixed[rows:, :] = jnp.zeros((PAD - rows, width), jnp.float32)
+    loads[1].wait()
+    for copy in back:
+        copy.wait_recv()
+
+    def project(dz, dx):
+        slot = links.slot(dz, dx)
+
+        def tile(i, _):
+            at = pl.ds(pl.multiple_of(i * 256, 256), 256)
+            left = every[slot, :, :, at].reshape(4 * HD, 256)
+            mixed[at, :] += lax.dot_general(
+                left, wo[slot], (((0,), (0,)), ((), ())), preferred_element_type=jnp.float32
+            )
+            return 0
+
+        lax.fori_loop(0, PAD // 256, tile, 0)
+
+    gather_tensor(links, lambda slot, lo, hi: every.at[slot, lo:hi], project)
+    loads[2].wait()
+    loads[3].wait()
+
+    def feed_forward(start, step):
+        def block(k, _):
+            slot = links.slot(start[0] + step[0] * k, start[1] + step[1] * k)
+            at = pl.ds(pl.multiple_of(slot * share, 32), share)
+            post[...] = layer_norm(mixed[at, :], gain[...]).astype(jnp.bfloat16)
+            up = jnp.dot(post[...], wu[...], preferred_element_type=jnp.float32)
+            hidden = jax.nn.gelu(up, approximate=True).astype(jnp.bfloat16)
+            down = jnp.dot(hidden, wd[...], preferred_element_type=jnp.float32)
+            term[slot] = down.astype(jnp.bfloat16)
+            return 0
+
+        lax.fori_loop(0, 2, block, 0)
+
+    first, second = reduce_tensor(links, term, stage, share, width, feed_forward)
+    at = pl.ds(pl.multiple_of(me * share, 32), share)
+    out_ref[me, :, 0 : 2 * quarter] = (mixed[at, 0 : 2 * quarter] + first).astype(jnp.bfloat16)
+    out_ref[me, :, 2 * quarter :] = (mixed[at, 2 * quarter :] + second).astype(jnp.bfloat16)
     gather_tensor(links, lambda slot, lo, hi: out_ref.at[slot, :, lo * quarter : hi * quarter])
 
 
-def finish(term, mixed):
-    parts, rows, cols = term.shape
-    copies = 40
+def tail(o, w_out, tokens, gain, w_up, w_down):
+    rows, cols = tokens.shape
+    share = PAD // 8
+    copies = 64
+    bf16 = jnp.bfloat16
+    anywhere = pl.BlockSpec(memory_space=pl.ANY)
     return pl.pallas_call(
-        finish_kernel,
-        out_shape=jax.ShapeDtypeStruct(term.shape, jnp.bfloat16),
-        in_specs=[FULL, FULL],
+        tail_kernel,
+        out_shape=jax.ShapeDtypeStruct((8, share, cols), bf16),
+        in_specs=[FULL, anywhere, anywhere, FULL, anywhere, anywhere],
         out_specs=FULL,
         scratch_shapes=[
-            pltpu.VMEM(term.shape, jnp.bfloat16),
-            pltpu.VMEM((17, rows, cols // 2), jnp.bfloat16),
+            pltpu.VMEM((8,) + o.shape, bf16),
+            pltpu.VMEM((PAD, cols), jnp.float32),
+            pltpu.VMEM((share, cols), bf16),
+            pltpu.VMEM((8, share, cols), bf16),
+            pltpu.VMEM((17, share, cols // 2), bf16),
+            pltpu.VMEM(w_out.shape, bf16),
+            pltpu.VMEM(tokens.shape, bf16),
+            pltpu.VMEM(w_up.shape, bf16),
+            pltpu.VMEM(w_down.shape, bf16),
             pltpu.SemaphoreType.DMA((copies,)),
             pltpu.SemaphoreType.DMA((copies,)),
+            pltpu.SemaphoreType.DMA((4,)),
         ],
-        compiler_params=pltpu.CompilerParams(collective_id=2, has_side_effects=True, vmem_limit_bytes=40 * 2**20),
-        name="finish",
-    )(term, mixed)
+        compiler_params=pltpu.CompilerParams(collective_id=1, has_side_effects=True, vmem_limit_bytes=48 * 2**20),
+        name="tail",
+    )(o, w_out, tokens, gain, w_up, w_down)
 
 
 def per_device(tokens, norm_gain, w_qkv, w_out, post_gain, w_up, w_down):
     rows, width = tokens.shape
     heads = w_qkv.shape[2] // HD
-    t = lax.axis_index("tensor")
     base = tokens.astype(jnp.float32)
     normed = layer_norm(base, norm_gain).astype(jnp.bfloat16)
     qkv = lax.dot_general(w_qkv, normed, (((0,), (1,)), ((), ())), preferred_element_type=jnp.float32)
@@ -531,19 +593,7 @@
     qkv = jnp.pad(qkv, ((0, 0), (0, 0), (0, PAD - rows))).reshape(3, heads, HD, PAD)
 
     o, w_out_all = attention(rows, qkv, w_out)
-    every = gather_heads(o).reshape(8 * heads * HD, PAD)
-    padded = jnp.pad(base, ((0, PAD - rows), (0, 0)))
-    mixed = padded + lax.dot_general(
-        every, w_out_all, (((0,), (0,)), ((), ())), preferred_element_type=jnp.float32
-    )
-    post = layer_norm(mixed, post_gain).astype(jnp.bfloat16)
-    hidden = jax.nn.gelu(
-        jnp.dot(post, w_up, preferred_element_type=jnp.float32), approximate=True
-    ).astype(jnp.bfloat16)
-    term = jnp.dot(hidden, w_down, preferred_element_type=jnp.float32).astype(jnp.bfloat16)
-    share = PAD // 8
-    mine = lax.dynamic_slice_in_dim(mixed, t * share, share, 0)
-    out = finish(term.reshape(8, share, width), mine)
+    out = tail(o, w_out_all.reshape(8, heads * HD, width), tokens, post_gain.reshape(1, width), w_up, w_down)
     return out.reshape(PAD, width)[:rows]
 
 

time: 256 us -> 240 us (0.938)
  matrix products: 15 us -> 1.67 us
  local copies, waits for them, and re-layouts: 8.64 us -> 2.97 us
  Pallas kernels: 228 us -> 232 us
    dot_general x2 -> x0, matrix products: 13.3 us -> none  [the longest x1 9.34 us: per_device(): jnp.dot(hidden, w_down, preferred_element_type=jnp.float32)]
    unnamed x20 -> x12, local copies, waits for them, and re-layouts: 5.96 us -> 1.38 us
    pallas_call x2 -> x1, Pallas kernels: 172 us -> 176 us  [tail(): pl.pallas_call(tail_kernel, out_shape=jax.ShapeDtypeStruct((8, share, col...]
where the time goes in v1:
time: 240 us
  Pallas kernels  232 us (97%)
  other arithmetic  3.04 us (1%)
  local copies, waits for them, and re-layouts  2.97 us (1%)
    pallas_call x1, Pallas kernels, tail(): pl.pallas_call(tail_kernel, out_shape=jax.ShapeDtypeStruct((8, share, col...  176 us
    pallas_call x1, Pallas kernels, attention(): pl.pallas_call(functools.partial(attend_kernel, rows), out_shape=(jax.Sha...  55.4 us

profile of v1, /device:TPU:0, one launch (start us, length us, event | category | flops | bytes accessed | tf_op | source)
XLA Modules:
  0.0 239.7 jit_solution(16740609256513939328)
XLA Ops:
  0.0 0.0 copy-start
  0.0 0.0 copy-start.1
  0.0 0.0 copy-start.5
  0.0 2.1 convert_reduce_fusion
  2.1 0.3 copy-done.1
  2.4 0.7 fusion.2
  3.1 0.0 copy-done
  3.2 0.0 copy-done.5
  3.2 0.0 copy-start.4
  3.2 1.7 fusion.5
  4.8 0.0 copy-done.4
  4.9 0.0 copy-start.2
  4.9 0.2 fusion.10
  5.1 0.1 pad.4
  5.2 0.8 copy-done.2
  5.9 55.4 %attend.1 = (f32[64,3072]{1,0:T(8,128)S(1)}, bf16[4,3,48,768]{3,2,1,0:T(8,128)(2,1)S(1)}, bf16[3,4,2,48,768]{4,3,2,1,0:T(8,128)(2,1)S(1)}, bf16[8,2,96,1536]{3,2,1,0:T(8,128)(2,1)}) custom-call(bf16[3,4,48,768]{3,2,1,0:T(8,128)(2,1)S(1)} %bitcast.11, bf16[2,96,1536]{2,1,0:T(8,128)(2,1)S(1)} %bitcast.12), custom_call_target="tpu_custom_call" | custom-call | tf_op jit(solution)/shard_map/attend/pallas_call | solution.py:258
  61.3 0.0 copy-start.3
  61.3 0.4 settle.1.o_ref
  61.7 0.3 copy-done.3
  62.0 176.2 %tail.1 = bf16[8,96,1536]{2,1,0:T(8,128)(2,1)S(1)} custom-call(bf16[4,48,768]{2,1,0:T(8,128)(2,1)S(1)} %settle.1.o_ref, bf16[8,192,1536]{2,1,0:T(8,128)(2,1)} %bitcast.13, bf16[720,1536]{1,0:T(8,128)(2,1)S(1)} %copy-done.1, f32[1,1536]{1,0:T(1,128)S(1)} %reshape.28.gain, bf16[1536,768]{1,0:T(8,128)(2,1)} %w_up.1, bf16[768,1536]{1,0:T(8,128)(2,1)} %w_down.1), custom_call_target="tpu_custom_call" | custom-call | tf_op jit(solution)/shard_map/tail/pallas_call | solution.py:561
  238.2 1.5 slice.4
  (3 shorter events, 0.0 us)
Async XLA Ops:
  0.0 3.1 %copy-start = (bf16[1536,3,192]{0,2,1:T(8,128)(2,1)S(1)}, bf16[1536,3,192]{0,2,1:T(8,128)(2,1)}, u32[]{:S(2)}) copy-start(bf16[1536,3,192]{0,2,1:T(8,128)(2,1)} %param.10) | copy-start | bytes 5308420
  0.0 2.4 %copy-start.1 = (bf16[720,1536]{1,0:T(8,128)(2,1)S(1)}, bf16[720,1536]{1,0:T(8,128)(2,1)}, u32[]{:S(2)}) copy-start(bf16[720,1536]{1,0:T(8,128)(2,1)} %tokens.1) | copy-start | bytes 6635524
  0.0 3.2 %copy-start.5 = (f32[1536]{0:T(1024)S(1)}, f32[1536]{0:T(1024)}, u32[]{:S(2)}) copy-start(f32[1536]{0:T(1024)} %param.9) | copy-start | bytes 18436
  3.2 1.7 copy-start.4
  4.9 1.1 copy-start.2
  61.3 0.7 copy-start.3

commit v2 on v1

--- a/solution.py
+++ b/solution.py
@@ -9,7 +9,7 @@
 
 HD = 48
 PAD = 768
-WIDE = 1024
+WIDE = PAD
 MESH = pl.DeviceIdType.MESH
 LOG2E = 1.4426950408889634
 LIMIT = 2.0**90
@@ -24,12 +24,22 @@
     return centred * lax.rsqrt(var + 1e-05) * gain
 
 
-def sweep(rows, blocks, queries, keys, vals, acc, probs, unroll, stage):
-    chunks = queries.shape[1] // WIDE
-    total = blocks * chunks
+def unit(i):
+    k = i - 9
+    b, c = i // 4, lax.rem(i, 4)
+    b, c = jnp.where(i < 32, i - 24, b), jnp.where(i < 32, 3, c)
+    b, c = jnp.where(i < 24, 7, b), jnp.where(i < 24, i - 21, c)
+    b, c = jnp.where(i < 21, 3, b), jnp.where(i < 21, i - 18, c)
+    b, c = jnp.where(i < 18, 4 + k // 3, b), jnp.where(i < 18, lax.rem(k, 3), c)
+    return jnp.where(i < 9, lax.rem(i, 3), b), jnp.where(i < 9, i // 3, c)
+
+
+def sweep(rows, queries, keys, vals, acc, probs, unroll, stages):
+    total = 64
 
     def place(i):
-        return i // chunks, pl.ds(pl.multiple_of(lax.rem(i, chunks) * WIDE, WIDE), WIDE)
+        b, c = unit(i)
+        return b, pl.ds(pl.multiple_of(c * WIDE, WIDE), WIDE)
 
     def scores(i, slot):
         b, cols = place(i)
@@ -40,14 +50,14 @@
         b, cols = place(i)
         acc[:, cols] += jnp.dot(vals[b], probs[slot], preferred_element_type=jnp.float32)
 
-    scores(0, 0)
+    scores(jnp.int32(0), 0)
 
     def body(j, _):
-        for k in range(total // unroll):
+        for k, stage in stages.items():
 
             @pl.when(j == k)
-            def _(k=k):
-                stage(k)
+            def _(stage=stage):
+                stage()
 
         for u in range(unroll):
             i = unroll * j + u
@@ -73,11 +83,18 @@
     vals[b, HD : HD + 16] = count
 
 
-def attend_kernel(rows, qkv, w_ref, acc, land, kvx, w_all, queries, keys, vals, probs, w_own, send, recv, local):
+def attend_kernel(
+    tokens, gain, w_in, w_own, acc, land, kvx, w_all, tok, normed, qkv, queries, keys, vals, probs, send, recv, local
+):
+    rows = tok.shape[0]
     width = queries.shape[1]
     seq, me = lax.axis_index("seq"), lax.axis_index("tensor")
     z, y, core = seq // 8, lax.rem(seq // 2, 4), lax.rem(seq, 2)
     links = Links(send, recv)
+    fetch = pltpu.make_async_copy(tokens, tok, local.at[0])
+    fetch.start()
+    keep = pltpu.make_async_copy(w_own, w_all.at[me], local.at[1])
+    keep.start()
 
     def on_seq(dz, dy, dc):
         return ((lax.rem(z + dz, 2) * 4 + lax.rem(y + dy, 4)) * 2 + lax.rem(core + dc, 2), me)
@@ -87,22 +104,33 @@
     peers += [(seq, links.slot(1, 0)), (seq, links.slot(0, 1)), (seq, links.slot(0, 3))]
     for peer in peers:
         pl.semaphore_signal(barrier, inc=1, device_id=peer, device_id_type=MESH)
+
+    step = rows // 5
+    normed[rows:PAD, :] = jnp.zeros((PAD - rows, normed.shape[1]), jnp.bfloat16)
+    fetch.wait()
+
+    def norm_rows(i, _):
+        at = pl.ds(pl.multiple_of(i * step, 16), step)
+        normed[at, :] = layer_norm(tok[at, :].astype(jnp.float32), gain[...]).astype(jnp.bfloat16)
+        return 0
+
+    lax.fori_loop(0, 5, norm_rows, 0)
+    span = w_in.shape[0] // 3
+    wide = lax.dot_general(w_in[...], normed[...], (((1,), (1,)), ((), ())), preferred_element_type=jnp.float32)
+    for p in range(3):
+        part = wide[p * span : (p + 1) * span]
+        if p == 0:
+            part = part * (LOG2E / HD**0.5)
+        qkv[p] = part.astype(jnp.bfloat16).reshape(4, HD, PAD)
     pl.semaphore_wait(barrier, 8)
 
     by_y = {}
-    for d in (2, 1, 3):
+    for d in (1, 3, 2):
         by_y[d] = links.start(lambda d=d: (qkv.at[:, lax.rem(y + d, 4)], land.at[d], on_seq(0, d, 0)))
-    to_core, to_far, far_core = {}, {}, {}
+    to_core, to_far, far_core, more = {}, {}, {}, {}
     to_core[0] = links.start(lambda: (qkv.at[1:3, y], kvx.at[0, 0], on_seq(0, 0, 1)))
     to_far[0] = links.start(lambda: (qkv.at[1:3, y], kvx.at[1, 0], on_seq(1, 0, 0)))
 
-    fetch = pltpu.make_async_copy(w_ref, w_own, local.at[0])
-    fetch.start()
-    land[0] = qkv[:, y]
-    load_block(rows, land.at[0, 1:3], 0, keys, vals)
-    fetch.wait()
-    keep = pltpu.make_async_copy(w_own, w_all.at[me], local.at[1])
-    keep.start()
     w_cols = w_own.shape[2] // 2
 
     def tensor_at(dz, dx):
@@ -127,28 +155,24 @@
 
     wz, wup, wdown = own_w(1, 0), own_w(0, 1), own_w(0, 3)
 
-    acc[...] = jnp.zeros_like(acc)
-    probs[:, rows:PAD, :] = jnp.zeros((2, PAD - rows, WIDE), jnp.bfloat16)
-    queries[HD:128, :] = jnp.zeros((128 - HD, width), jnp.bfloat16)
-    queries[0:HD, 0:PAD] = land[0, 0]
-    for i in (1, 2, 3):
+    def set_queries(i):
+        cols = slice(i * PAD, (i + 1) * PAD)
+        queries[0:HD, cols] = land[ORDER[i], 0]
+        queries[HD:128, cols] = jnp.zeros((128 - HD, PAD), jnp.bfloat16)
+        s = jnp.dot(keys[0, 0:rows], queries[:, cols], preferred_element_type=jnp.float32)
+        top = jnp.max(s.reshape(rows // 8, 8, PAD), axis=0)
+        top = jnp.max(top, axis=0, keepdims=True)
+        first = lax.broadcasted_iota(jnp.int32, (16, PAD), 0) == 0
+        shift = jnp.where(first, jnp.broadcast_to(-top, (16, PAD)), 0.0)
+        queries[HD : HD + 16, cols] = shift.astype(jnp.bfloat16)
+
+    def arrive(i):
         d = ORDER[i]
         by_y[d].wait_recv()
-        to_core[d] = links.start(lambda d=d: (land.at[d, 1:3], kvx.at[0, d], on_seq(0, 0, 1)))
-        to_far[d] = links.start(lambda d=d: (land.at[d, 1:3], kvx.at[1, d], on_seq(1, 0, 0)))
+        to_core[d] = links.start(lambda: (land.at[d, 1:3], kvx.at[0, d], on_seq(0, 0, 1)))
+        to_far[d] = links.start(lambda: (land.at[d, 1:3], kvx.at[1, d], on_seq(1, 0, 0)))
         load_block(rows, land.at[d, 1:3], i, keys, vals)
-        queries[0:HD, d * PAD : (d + 1) * PAD] = land[d, 0]
-
-    for c in range(width // WIDE):
-        cols = slice(c * WIDE, (c + 1) * WIDE)
-        s = jnp.dot(keys[0, 0:rows], queries[:, cols], preferred_element_type=jnp.float32)
-        top = jnp.max(s.reshape(rows // 8, 8, WIDE), axis=0)
-        top = jnp.max(top, axis=0, keepdims=True)
-        first = lax.broadcasted_iota(jnp.int32, (16, WIDE), 0) == 0
-        shift = jnp.where(first, jnp.broadcast_to(-top, (16, WIDE)), 0.0)
-        queries[HD : HD + 16, cols] = shift.astype(jnp.bfloat16)
-
-    more = {}
+        set_queries(i)
 
     def take(block):
         group, d = block // 4, ORDER[block % 4]
@@ -156,37 +180,62 @@
             to_core[d].wait_recv()
         elif group == 2:
             to_far[d].wait_recv()
-            far_core[d] = links.start(lambda d=d: (kvx.at[1, d], kvx.at[2, d], on_seq(0, 0, 1)))
+            far_core[d] = links.start(lambda: (kvx.at[1, d], kvx.at[2, d], on_seq(0, 0, 1)))
         elif group == 3:
             far_core[d].wait_recv()
         load_block(rows, kvx.at[group - 1, d], block, keys, vals)
 
     others = [(0, 1), (0, 2), (0, 3), (1, 0), (1, 1), (1, 2), (1, 3)]
 
-    def stage(j):
-        for block in (2 * j + 1, 2 * j + 2):
-            if 4 <= block < 16:
-                take(block)
-        if j == 1:
-            wz.wait_recv()
-            more["zup"] = pass_w((1, 0), 0, 2, 0, 1)
-            more["zdown"] = pass_w((1, 0), 0, 2, 0, 3)
-            wup.wait_recv()
-            more["r0"] = pass_w((0, 3), 0, 1, 0, 1)
-            wdown.wait_recv()
-            more["r1"] = pass_w((0, 1), 1, 2, 0, 3)
-        if j == 3:
-            more["zup"].wait_recv()
-            more["q0"] = pass_w((1, 3), 0, 1, 0, 1)
-            more["zdown"].wait_recv()
-            more["q1"] = pass_w((1, 1), 1, 2, 0, 3)
-        if j == 6:
-            for name in ("r0", "r1", "q0", "q1"):
-                more[name].wait_recv()
-            for dz, dx in others:
-                more[dz, dx] = swap_w((dz, dx))
-
-    sweep(rows, 16, queries, keys, vals, acc, probs, 6, stage)
+    def w_first():
+        wz.wait_recv()
+        more["zup"] = pass_w((1, 0), 0, 2, 0, 1)
+        more["zdown"] = pass_w((1, 0), 0, 2, 0, 3)
+        wup.wait_recv()
+        more["r0"] = pass_w((0, 3), 0, 1, 0, 1)
+        wdown.wait_recv()
+        more["r1"] = pass_w((0, 1), 1, 2, 0, 3)
+
+    def w_second():
+        more["zup"].wait_recv()
+        more["q0"] = pass_w((1, 3), 0, 1, 0, 1)
+        more["zdown"].wait_recv()
+        more["q1"] = pass_w((1, 1), 1, 2, 0, 3)
+
+    def w_third():
+        for name in ("r0", "r1", "q0", "q1"):
+            more[name].wait_recv()
+        for pair in others:
+            more[pair] = swap_w(pair)
+
+    def both(*steps):
+        def run():
+            for function, *args in steps:
+                function(*args)
+
+        return run
+
+    stages = {
+        0: both((arrive, 1), (arrive, 2)),
+        2: both((take, 4), (take, 5)),
+        3: both((take, 6),),
+        4: both((arrive, 3), (w_first,)),
+        5: both((take, 7),),
+        7: both((take, 8),),
+        8: both((take, 9), (w_second,)),
+        9: both((take, 10),),
+        10: both((take, 11),),
+        11: both((take, 12),),
+        12: both((take, 13), (w_third,)),
+        13: both((take, 14),),
+        14: both((take, 15),),
+    }
+    land[0] = qkv[:, y]
+    load_block(rows, land.at[0, 1:3], 0, keys, vals)
+    acc[...] = jnp.zeros_like(acc)
+    probs[:, rows:PAD, :] = jnp.zeros((2, PAD - rows, WIDE), jnp.bfloat16)
+    set_queries(0)
+    sweep(rows, queries, keys, vals, acc, probs, 4, stages)
     keep.wait()
     for pair in others:
         more[pair].wait_recv()
@@ -200,8 +249,8 @@
     again = jnp.max(fits) > 0.5
 
     def write(sums):
-        for d in range(4):
-            cols = slice(d * PAD, (d + 1) * PAD)
+        for i, d in enumerate(ORDER):
+            cols = slice(i * PAD, (i + 1) * PAD)
             o_ref[d] = (sums[0:HD, cols] / sums[HD : HD + 1, cols]).astype(jnp.bfloat16)
 
     @pl.when(jnp.logical_not(again))
@@ -211,8 +260,8 @@
     @pl.when(again)
     def _():
         queries[HD:128, :] = jnp.zeros((128 - HD, width), jnp.bfloat16)
-        for d in range(4):
-            queries[0:HD, d * PAD : (d + 1) * PAD] = land[d, 0]
+        for i, d in enumerate(ORDER):
+            queries[0:HD, i * PAD : (i + 1) * PAD] = land[d, 0]
         probs[rows:PAD, :] = jnp.zeros((PAD - rows, 256), jnp.bfloat16)
         acc[...] = jnp.zeros_like(acc)
 
@@ -244,7 +293,8 @@
         write(acc)
 
 
-def attention(rows, qkv, w_out):
+def attention(tokens, gain, w_qkv, w_out):
+    rows, features = tokens.shape
     width = 4 * PAD
     bf16 = jnp.bfloat16
     half, cols = w_out.shape[0] // 2, w_out.shape[1]
@@ -256,26 +306,35 @@
     ]
     anywhere = pl.BlockSpec(memory_space=pl.ANY)
     acc, land, kvx, w_all = pl.pallas_call(
-        functools.partial(attend_kernel, rows),
+        attend_kernel,
         out_shape=(
             jax.ShapeDtypeStruct((HD + 16, width), jnp.float32),
             jax.ShapeDtypeStruct((4, 3, HD, PAD), bf16),
             jax.ShapeDtypeStruct((3, 4, 2, HD, PAD), bf16),
             jax.ShapeDtypeStruct((8, 2, half, cols), bf16),
         ),
-        in_specs=[FULL, anywhere],
+        in_specs=[anywhere, FULL, FULL, FULL],
         out_specs=(FULL, FULL, FULL, anywhere),
-        scratch_shapes=tables
+        scratch_shapes=[
+            pltpu.VMEM(tokens.shape, bf16),
+            pltpu.VMEM((PAD, features), bf16),
+            pltpu.VMEM((3, 4, HD, PAD), bf16),
+        ]
+        + tables
         + [
             pltpu.VMEM((2, PAD, WIDE), bf16),
-            pltpu.VMEM((2, half, cols), bf16),
             pltpu.SemaphoreType.DMA((n,)),
             pltpu.SemaphoreType.DMA((n,)),
             pltpu.SemaphoreType.DMA((2,)),
         ],
         compiler_params=pltpu.CompilerParams(collective_id=0, has_side_effects=True, vmem_limit_bytes=48 * 2**20),
         name="attend",
-    )(qkv, w_out.reshape(2, half, cols))
+    )(
+        tokens,
+        gain.reshape(1, features),
+        jnp.transpose(w_qkv, (1, 2, 0)).reshape(3 * w_qkv.shape[2], features),
+        w_out.reshape(2, half, cols),
+    )
     o = pl.pallas_call(
         functools.partial(settle_kernel, rows),
         out_shape=jax.ShapeDtypeStruct((4, HD, PAD), bf16),
@@ -484,7 +543,7 @@
 
 
 def tail_kernel(
-    o_ref, w_out, tokens, gain, w_up, w_down, out_ref, every, mixed, post, term, stage, wo, tok, wu, wd, send, recv, local
+    o_ref, w_out, tok, gain, w_up, w_down, out_ref, every, mixed, post, term, stage, wo, wu, wd, send, recv, local
 ):
     links = Links(send, recv)
     seq, me = links.seq, links.me
@@ -494,7 +553,7 @@
     rows = tok.shape[0]
     loads = [
         pltpu.make_async_copy(src, dst, local.at[i])
-        for i, (src, dst) in enumerate(((tokens, tok), (w_out, wo), (w_up, wu), (w_down, wd)))
+        for i, (src, dst) in enumerate(((w_out, wo), (w_up, wu), (w_down, wd)))
     ]
     for load in loads:
         load.start()
@@ -508,10 +567,9 @@
     links.barrier(3)
     back = [links.start(lambda d=d: (o_ref.at[d], every.at[me, y], at_y(4 - d))) for d in (2, 1, 3)]
     every[me, y] = o_ref[0]
-    loads[0].wait()
     mixed[0:rows, :] = tok[...].astype(jnp.float32)
     mixed[rows:, :] = jnp.zeros((PAD - rows, width), jnp.float32)
-    loads[1].wait()
+    loads[0].wait()
     for copy in back:
         copy.wait_recv()
 
@@ -529,8 +587,8 @@
         lax.fori_loop(0, PAD // 256, tile, 0)
 
     gather_tensor(links, lambda slot, lo, hi: every.at[slot, lo:hi], project)
+    loads[1].wait()
     loads[2].wait()
-    loads[3].wait()
 
     def feed_forward(start, step):
         def block(k, _):
@@ -561,7 +619,7 @@
     return pl.pallas_call(
         tail_kernel,
         out_shape=jax.ShapeDtypeStruct((8, share, cols), bf16),
-        in_specs=[FULL, anywhere, anywhere, FULL, anywhere, anywhere],
+        in_specs=[FULL, anywhere, FULL, FULL, anywhere, anywhere],
         out_specs=FULL,
         scratch_shapes=[
             pltpu.VMEM((8,) + o.shape, bf16),
@@ -570,12 +628,11 @@
             pltpu.VMEM((8, share, cols), bf16),
             pltpu.VMEM((17, share, cols // 2), bf16),
             pltpu.VMEM(w_out.shape, bf16),
-            pltpu.VMEM(tokens.shape, bf16),
             pltpu.VMEM(w_up.shape, bf16),
             pltpu.VMEM(w_down.shape, bf16),
             pltpu.SemaphoreType.DMA((copies,)),
             pltpu.SemaphoreType.DMA((copies,)),
-            pltpu.SemaphoreType.DMA((4,)),
+            pltpu.SemaphoreType.DMA((3,)),
         ],
         compiler_params=pltpu.CompilerParams(collective_id=1, has_side_effects=True, vmem_limit_bytes=48 * 2**20),
         name="tail",
@@ -585,14 +642,7 @@
 def per_device(tokens, norm_gain, w_qkv, w_out, post_gain, w_up, w_down):
     rows, width = tokens.shape
     heads = w_qkv.shape[2] // HD
-    base = tokens.astype(jnp.float32)
-    normed = layer_norm(base, norm_gain).astype(jnp.bfloat16)
-    qkv = lax.dot_general(w_qkv, normed, (((0,), (1,)), ((), ())), preferred_element_type=jnp.float32)
-    factor = jnp.array([LOG2E / HD**0.5, 1.0, 1.0], jnp.float32)[:, None, None]
-    qkv = (qkv * factor).astype(jnp.bfloat16)
-    qkv = jnp.pad(qkv, ((0, 0), (0, 0), (0, PAD - rows))).reshape(3, heads, HD, PAD)
-
-    o, w_out_all = attention(rows, qkv, w_out)
+    o, w_out_all = attention(tokens, norm_gain, w_qkv, w_out)
     out = tail(o, w_out_all.reshape(8, heads * HD, width), tokens, post_gain.reshape(1, width), w_up, w_down)
     return out.reshape(PAD, width)[:rows]
 

time: 240 us -> 238 us (level); the launches traced: 240 us -> 235 us
  other arithmetic: 3.04 us -> 0 us
  local copies, waits for them, and re-layouts: 2.97 us -> 5.99 us
  Pallas kernels: 232 us -> 229 us
    reduce_sum x2 -> x0, other arithmetic: 2.84 us -> none  [the longest x1 2.13 us: layer_norm(): mean = jnp.mean(values, axis=-1, keepdims=True)]
where the time goes in v2:
time: 238 us; the launch traced here: 235 us
  Pallas kernels  229 us (96%)
  local copies, waits for them, and re-layouts  5.99 us (3%)
    pallas_call x1, Pallas kernels, tail(): pl.pallas_call(tail_kernel, out_shape=jax.ShapeDtypeStruct((8, share, col...  175 us
    pallas_call x1, Pallas kernels, attention(): pl.pallas_call(attend_kernel, out_shape=(jax.ShapeDtypeStruct((HD + 16, w...  53.9 us

profile of v2, /device:TPU:0, one launch (start us, length us, event | category | flops | bytes accessed | tf_op | source)
XLA Modules:
  0.0 235.1 jit_solution(2788750417746598803)
XLA Ops:
  0.0 0.7 reshape.15.gain
  0.7 0.0 copy-start.1
  0.7 1.5 copy-done.1
  2.2 0.0 copy-start.2
  2.2 1.1 copy-done.2
  3.2 53.9 %attend.1 = (f32[64,3072]{1,0:T(8,128)S(1)}, bf16[4,3,48,768]{3,2,1,0:T(8,128)(2,1)S(1)}, bf16[3,4,2,48,768]{4,3,2,1,0:T(8,128)(2,1)S(1)}, bf16[8,2,96,1536]{3,2,1,0:T(8,128)(2,1)}) custom-call(bf16[720,1536]{1,0:T(8,128)(2,1)} %tok.1, f32[1,1536]{1,0:T(1,128)S(1)} %reshape.15.gain, bf16[576,1536]{1,0:T(8,128)(2,1)S(1)} %bitcast.7, ...), custom_call_target="tpu_custom_call" | custom-call | tf_op jit(solution)/shard_map/attend/pallas_call | solution.py:308
  57.2 0.0 copy-start.3
  57.2 0.0 copy-start
  57.2 0.4 settle.1.o_ref
  57.6 0.3 copy-done.3
  57.9 0.9 copy-done
  58.8 174.8 %tail.1 = bf16[8,96,1536]{2,1,0:T(8,128)(2,1)S(1)} custom-call(bf16[4,48,768]{2,1,0:T(8,128)(2,1)S(1)} %settle.1.o_ref, bf16[8,192,1536]{2,1,0:T(8,128)(2,1)} %bitcast.9, bf16[720,1536]{1,0:T(8,128)(2,1)S(1)} %copy-done, f32[1,1536]{1,0:T(1,128)S(1)} %reshape.18.gain, bf16[1536,768]{1,0:T(8,128)(2,1)} %w_up.1, bf16[768,1536]{1,0:T(8,128)(2,1)} %w_down.1), custom_call_target="tpu_custom_call" | custom-call | tf_op jit(solution)/shard_map/tail/pallas_call | solution.py:619
  233.6 1.5 slice.4
  (1 shorter events, 0.0 us)
Async XLA Ops:
  0.7 1.5 copy-start.1
  2.2 1.1 copy-start.2
  57.2 0.7 copy-start.3
  57.2 1.6 copy-start

commit v3 on v2

--- a/solution.py
+++ b/solution.py
@@ -24,49 +24,43 @@
     return centred * lax.rsqrt(var + 1e-05) * gain
 
 
-def unit(i):
-    k = i - 9
-    b, c = i // 4, lax.rem(i, 4)
-    b, c = jnp.where(i < 32, i - 24, b), jnp.where(i < 32, 3, c)
-    b, c = jnp.where(i < 24, 7, b), jnp.where(i < 24, i - 21, c)
-    b, c = jnp.where(i < 21, 3, b), jnp.where(i < 21, i - 18, c)
-    b, c = jnp.where(i < 18, 4 + k // 3, b), jnp.where(i < 18, lax.rem(k, 3), c)
-    return jnp.where(i < 9, lax.rem(i, 3), b), jnp.where(i < 9, i // 3, c)
-
-
-def sweep(rows, queries, keys, vals, acc, probs, unroll, stages):
-    total = 64
-
-    def place(i):
-        b, c = unit(i)
-        return b, pl.ds(pl.multiple_of(c * WIDE, WIDE), WIDE)
-
-    def scores(i, slot):
-        b, cols = place(i)
-        s = jnp.dot(keys[b, 0:rows], queries[:, cols], preferred_element_type=jnp.float32)
-        probs[slot, 0:rows, :] = jnp.exp2(s).astype(jnp.bfloat16)
-
-    def product(i, slot):
-        b, cols = place(i)
+def wide_row(ref):
+    return jnp.concatenate([ref[k : k + 1, :] for k in range(ref.shape[0])], axis=1)
+
+
+EARLY = [(b, c) for b in (0, 1, 2, 4, 5, 6, 3, 7) for c in range(3)] + [(b, 3) for b in range(8)]
+
+
+def sweep(rows, queries, keys, vals, acc, probs, early, late):
+    def scores(unit, slot):
+        b, c = unit
+        cols = slice(c * WIDE, (c + 1) * WIDE)
+        cut = rows // 32 * 16
+        for lo, hi in ((0, cut), (cut, rows)):
+            s = jnp.dot(keys[b, lo:hi], queries[:, cols], preferred_element_type=jnp.float32)
+            probs[slot, lo:hi, :] = jnp.exp2(s).astype(jnp.bfloat16)
+
+    def product(unit, slot):
+        b, c = unit
+        cols = slice(c * WIDE, (c + 1) * WIDE)
         acc[:, cols] += jnp.dot(vals[b], probs[slot], preferred_element_type=jnp.float32)
 
-    scores(jnp.int32(0), 0)
+    scores(EARLY[0], 0)
+    order = EARLY + [(8, 0)]
+    for n, pair in enumerate(EARLY):
+        if n + 1 in early:
+            early[n + 1]()
+        scores(order[n + 1], (n + 1) % 2)
+        product(pair, n % 2)
 
     def body(j, _):
-        for k, stage in stages.items():
-
-            @pl.when(j == k)
-            def _(stage=stage):
-                stage()
-
-        for u in range(unroll):
-            i = unroll * j + u
-            ahead = i + 1 if u < unroll - 1 else jnp.minimum(i + 1, total - 1)
-            scores(ahead, (u + 1) % 2)
-            product(i, u % 2)
+        late(j)
+        for c in range(4):
+            scores((8 + j, c + 1) if c < 3 else (jnp.minimum(9 + j, 15), 0), (c + 1) % 2)
+            product((8 + j, c), c % 2)
         return 0
 
-    lax.fori_loop(0, total // unroll, body, 0)
+    lax.fori_loop(0, 8, body, 0)
 
 
 ORDER = (0, 1, 3, 2)
@@ -84,17 +78,31 @@
 
 
 def attend_kernel(
-    tokens, gain, w_in, w_own, acc, land, kvx, w_all, tok, normed, qkv, queries, keys, vals, probs, send, recv, local
+    tokens, gain, w_in, w_ref, acc, land_out, kvx_out, w_all,
+    tok, wq, w_own, normed, qkv, land, kvx, queries, keys, vals, probs, send, recv, local,
 ):
     rows = tok.shape[0]
     width = queries.shape[1]
     seq, me = lax.axis_index("seq"), lax.axis_index("tensor")
     z, y, core = seq // 8, lax.rem(seq // 2, 4), lax.rem(seq, 2)
     links = Links(send, recv)
-    fetch = pltpu.make_async_copy(tokens, tok, local.at[0])
-    fetch.start()
-    keep = pltpu.make_async_copy(w_own, w_all.at[me], local.at[1])
-    keep.start()
+    fetch = [
+        pltpu.make_async_copy(src, dst, local.at[i])
+        for i, (src, dst) in enumerate(((tokens, tok), (w_in, wq), (w_ref, w_own)))
+    ]
+    for copy in fetch:
+        copy.start()
+
+    def keep(i):
+        src, dst = (
+            (w_own, w_all.at[me]),
+            (land, land_out),
+            (kvx.at[0], kvx_out.at[0]),
+            (kvx.at[1], kvx_out.at[1]),
+            (kvx.at[2], kvx_out.at[2]),
+        )[i]
+        return pltpu.make_async_copy(src, dst, local.at[3 + i])
+
 
     def on_seq(dz, dy, dc):
         return ((lax.rem(z + dz, 2) * 4 + lax.rem(y + dy, 4)) * 2 + lax.rem(core + dc, 2), me)
@@ -107,16 +115,19 @@
 
     step = rows // 5
     normed[rows:PAD, :] = jnp.zeros((PAD - rows, normed.shape[1]), jnp.bfloat16)
-    fetch.wait()
+    fetch[0].wait()
+
+    scale = wide_row(gain)
 
     def norm_rows(i, _):
         at = pl.ds(pl.multiple_of(i * step, 16), step)
-        normed[at, :] = layer_norm(tok[at, :].astype(jnp.float32), gain[...]).astype(jnp.bfloat16)
+        normed[at, :] = layer_norm(tok[at, :].astype(jnp.float32), scale).astype(jnp.bfloat16)
         return 0
 
     lax.fori_loop(0, 5, norm_rows, 0)
+    fetch[1].wait()
     span = w_in.shape[0] // 3
-    wide = lax.dot_general(w_in[...], normed[...], (((1,), (1,)), ((), ())), preferred_element_type=jnp.float32)
+    wide = lax.dot_general(wq[...], normed[...], (((1,), (1,)), ((), ())), preferred_element_type=jnp.float32)
     for p in range(3):
         part = wide[p * span : (p + 1) * span]
         if p == 0:
@@ -131,6 +142,8 @@
     to_core[0] = links.start(lambda: (qkv.at[1:3, y], kvx.at[0, 0], on_seq(0, 0, 1)))
     to_far[0] = links.start(lambda: (qkv.at[1:3, y], kvx.at[1, 0], on_seq(1, 0, 0)))
 
+    fetch[2].wait()
+    keep(0).start()
     w_cols = w_own.shape[2] // 2
 
     def tensor_at(dz, dx):
@@ -215,34 +228,62 @@
 
         return run
 
-    stages = {
-        0: both((arrive, 1), (arrive, 2)),
-        2: both((take, 4), (take, 5)),
-        3: both((take, 6),),
-        4: both((arrive, 3), (w_first,)),
-        5: both((take, 7),),
-        7: both((take, 8),),
-        8: both((take, 9), (w_second,)),
-        9: both((take, 10),),
-        10: both((take, 11),),
-        11: both((take, 12),),
-        12: both((take, 13), (w_third,)),
-        13: both((take, 14),),
-        14: both((take, 15),),
+    def store(i):
+        keep(i).start()
+
+    early = {
+        1: both((arrive, 1), (arrive, 2)),
+        9: both((take, 4),),
+        12: both((take, 5),),
+        15: both((take, 6),),
+        18: both((arrive, 3), (w_first,), (store, 1)),
+        21: both((take, 7), (store, 2)),
+        32: both((take, 8),),
     }
+
+    def landed(block):
+        group, d = block // 4, ORDER[block % 4]
+        if group == 2:
+            to_far[d].wait_recv()
+            far_core[d] = links.start(lambda: (kvx.at[1, d], kvx.at[2, d], on_seq(0, 0, 1)))
+        else:
+            far_core[d].wait_recv()
+
+    def late(j):
+        for k in range(7):
+
+            @pl.when(j == k)
+            def _(k=k):
+                landed(9 + k)
+                if k == 2:
+                    store(3)
+                if k == 6:
+                    store(4)
+                if k == 1:
+                    w_second()
+                if k == 4:
+                    w_third()
+
+        block = jnp.minimum(9 + j, 15)
+        far = (block >= 12).astype(jnp.int32)
+        i = block - 8 - 4 * far
+        d = i + (i == 2).astype(jnp.int32) - (i == 3).astype(jnp.int32)
+        load_block(rows, kvx.at[1 + far, d], block, keys, vals)
+
     land[0] = qkv[:, y]
     load_block(rows, land.at[0, 1:3], 0, keys, vals)
     acc[...] = jnp.zeros_like(acc)
     probs[:, rows:PAD, :] = jnp.zeros((2, PAD - rows, WIDE), jnp.bfloat16)
     set_queries(0)
-    sweep(rows, queries, keys, vals, acc, probs, 4, stages)
-    keep.wait()
+    sweep(rows, queries, keys, vals, acc, probs, early, late)
+    for i in range(5):
+        keep(i).wait()
     for pair in others:
         more[pair].wait_recv()
     links.drain()
 
 
-def settle_kernel(rows, acc_in, land, kvx, o_ref, queries, keys, vals, probs, acc):
+def settle_kernel(rows, acc_in, land_ref, kvx_ref, o_ref, land, kvx, queries, keys, vals, probs, acc, local):
     width = acc_in.shape[1]
     total = acc_in[HD : HD + 1, :]
     fits = jnp.where((total < LIMIT) & (total > FLOOR), 0.0, 1.0)
@@ -259,6 +300,14 @@
 
     @pl.when(again)
     def _():
+        loads = [
+            pltpu.make_async_copy(land_ref, land, local.at[0]),
+            pltpu.make_async_copy(kvx_ref, kvx, local.at[1]),
+        ]
+        for load in loads:
+            load.start()
+        for load in loads:
+            load.wait()
         queries[HD:128, :] = jnp.zeros((128 - HD, width), jnp.bfloat16)
         for i, d in enumerate(ORDER):
             queries[0:HD, i * PAD : (i + 1) * PAD] = land[d, 0]
@@ -304,6 +353,7 @@
         pltpu.VMEM((16, PAD, 128), bf16),
         pltpu.VMEM((16, HD + 16, PAD), bf16),
     ]
+    blocks = [pltpu.VMEM((4, 3, HD, PAD), bf16), pltpu.VMEM((3, 4, 2, HD, PAD), bf16)]
     anywhere = pl.BlockSpec(memory_space=pl.ANY)
     acc, land, kvx, w_all = pl.pallas_call(
         attend_kernel,
@@ -313,35 +363,44 @@
             jax.ShapeDtypeStruct((3, 4, 2, HD, PAD), bf16),
             jax.ShapeDtypeStruct((8, 2, half, cols), bf16),
         ),
-        in_specs=[anywhere, FULL, FULL, FULL],
-        out_specs=(FULL, FULL, FULL, anywhere),
+        in_specs=[anywhere, FULL, anywhere, anywhere],
+        out_specs=(FULL, anywhere, anywhere, anywhere),
         scratch_shapes=[
             pltpu.VMEM(tokens.shape, bf16),
+            pltpu.VMEM((3 * w_qkv.shape[2], features), bf16),
+            pltpu.VMEM((2, half, cols), bf16),
             pltpu.VMEM((PAD, features), bf16),
             pltpu.VMEM((3, 4, HD, PAD), bf16),
         ]
+        + blocks
         + tables
         + [
             pltpu.VMEM((2, PAD, WIDE), bf16),
             pltpu.SemaphoreType.DMA((n,)),
             pltpu.SemaphoreType.DMA((n,)),
-            pltpu.SemaphoreType.DMA((2,)),
+            pltpu.SemaphoreType.DMA((8,)),
         ],
-        compiler_params=pltpu.CompilerParams(collective_id=0, has_side_effects=True, vmem_limit_bytes=48 * 2**20),
+        compiler_params=pltpu.CompilerParams(collective_id=0, has_side_effects=True, vmem_limit_bytes=60 * 2**20),
         name="attend",
     )(
         tokens,
-        gain.reshape(1, features),
+        gain.reshape(features // 128, 128),
         jnp.transpose(w_qkv, (1, 2, 0)).reshape(3 * w_qkv.shape[2], features),
         w_out.reshape(2, half, cols),
     )
     o = pl.pallas_call(
         functools.partial(settle_kernel, rows),
         out_shape=jax.ShapeDtypeStruct((4, HD, PAD), bf16),
-        in_specs=[FULL] * 3,
+        in_specs=[FULL, anywhere, anywhere],
         out_specs=FULL,
-        scratch_shapes=tables + [pltpu.VMEM((PAD, 256), bf16), pltpu.VMEM((HD + 16, width), jnp.float32)],
-        compiler_params=pltpu.CompilerParams(vmem_limit_bytes=40 * 2**20),
+        scratch_shapes=blocks
+        + tables
+        + [
+            pltpu.VMEM((PAD, 256), bf16),
+            pltpu.VMEM((HD + 16, width), jnp.float32),
+            pltpu.SemaphoreType.DMA((2,)),
+        ],
+        compiler_params=pltpu.CompilerParams(vmem_limit_bytes=60 * 2**20),
         name="settle",
     )(acc, land, kvx)
     return o, w_all.reshape(16 * half, cols)
@@ -403,7 +462,7 @@
         self.make().wait_recv()
 
 
-def gather_tensor(links, piece, ready=lambda dz, dx: None):
+def gather_tensor(links, piece, ready=lambda dz, dx: None, between=lambda: None):
     s = links.slot
     put = links.put
 
@@ -413,11 +472,12 @@
 
     me = s(0, 0)
     a_z = pass_on(me, 0, 2, 1, 0)
+    a_up = pass_on(me, 0, 2, 0, 1)
+    a_down = pass_on(me, 0, 2, 0, 3)
+    between()
     b_up = pass_on(me, 2, 4, 0, 1)
     b_down = pass_on(me, 2, 4, 0, 3)
     b_z = pass_on(me, 2, 4, 1, 0)
-    a_up = pass_on(me, 0, 2, 0, 1)
-    a_down = pass_on(me, 0, 2, 0, 3)
     ready(0, 0)
     b_up.wait_recv()
     r2 = pass_on(s(0, 3), 2, 3, 0, 1)
@@ -500,21 +560,21 @@
         add_into(s(dz, 1), 1, 2, got(6 + j, 0, 1))
         near[dz, 1] = put(q(s(dz, 1), 0, 2), land(10 + j, 2), 0, 1)
 
-    make((1, 2), (1, 0))
+    make((1, 2), (0, 2))
     cross(0, 2)
     far(0, 1)
     far(1, 0)
-    make((1, 1), (0, 2))
+    make((1, 1), (1, 3))
     cross(1, 1)
     cross(2, 3)
     relay(0, 1)
-    make((0, 1), (0, 2))
+    make((0, 1), (0, 3))
     relay(1, 0)
     zb[2].wait_recv()
     add_into(s(0, 2), 2, 4, got(0, 0, 2))
     fb0 = put(q(s(0, 2), 2, 3), land(12, 1), 0, 3)
     fb1 = put(q(s(0, 2), 3, 4), land(13, 1), 0, 1)
-    make((1, 0), (1, 0))
+    make((1, 0), (0, 0))
     cross(3, 0)
     zb[1].wait_recv()
     zb[3].wait_recv()
@@ -534,16 +594,18 @@
     near[0, 1].wait_recv()
     za.wait_recv()
     first = val(s(0, 0), 0, 2) + got(9, 0, 2) + got(11, 0, 2) + got(14, 0, 2)
-    zb[0].wait_recv()
-    nb3.wait_recv()
-    nb1.wait_recv()
-    second = val(s(0, 0), 2, 4) + got(3, 0, 2) + got(15, 0, 2) + got(16, 0, 2)
-    links.drain()
+
+    def second():
+        zb[0].wait_recv()
+        nb3.wait_recv()
+        nb1.wait_recv()
+        return val(s(0, 0), 2, 4) + got(3, 0, 2) + got(15, 0, 2) + got(16, 0, 2)
+
     return first, second
 
 
 def tail_kernel(
-    o_ref, w_out, tok, gain, w_up, w_down, out_ref, every, mixed, post, term, stage, wo, wu, wd, send, recv, local
+    o_ref, w_out, tokens, gain, w_up, w_down, out_ref, every, mixed, post, term, stage, tok, wo, wu, wd, send, recv, local
 ):
     links = Links(send, recv)
     seq, me = links.seq, links.me
@@ -553,7 +615,7 @@
     rows = tok.shape[0]
     loads = [
         pltpu.make_async_copy(src, dst, local.at[i])
-        for i, (src, dst) in enumerate(((w_out, wo), (w_up, wu), (w_down, wd)))
+        for i, (src, dst) in enumerate(((tokens, tok), (w_out, wo), (w_up, wu), (w_down, wd)))
     ]
     for load in loads:
         load.start()
@@ -567,9 +629,10 @@
     links.barrier(3)
     back = [links.start(lambda d=d: (o_ref.at[d], every.at[me, y], at_y(4 - d))) for d in (2, 1, 3)]
     every[me, y] = o_ref[0]
+    loads[0].wait()
     mixed[0:rows, :] = tok[...].astype(jnp.float32)
     mixed[rows:, :] = jnp.zeros((PAD - rows, width), jnp.float32)
-    loads[0].wait()
+    loads[1].wait()
     for copy in back:
         copy.wait_recv()
 
@@ -587,27 +650,32 @@
         lax.fori_loop(0, PAD // 256, tile, 0)
 
     gather_tensor(links, lambda slot, lo, hi: every.at[slot, lo:hi], project)
-    loads[1].wait()
     loads[2].wait()
-
-    def feed_forward(start, step):
-        def block(k, _):
-            slot = links.slot(start[0] + step[0] * k, start[1] + step[1] * k)
+    loads[3].wait()
+
+    scale = wide_row(gain)
+
+    def feed_forward(*pair):
+        slots = [links.slot(*block) for block in pair]
+        for k, slot in enumerate(slots):
             at = pl.ds(pl.multiple_of(slot * share, 32), share)
-            post[...] = layer_norm(mixed[at, :], gain[...]).astype(jnp.bfloat16)
-            up = jnp.dot(post[...], wu[...], preferred_element_type=jnp.float32)
-            hidden = jax.nn.gelu(up, approximate=True).astype(jnp.bfloat16)
-            down = jnp.dot(hidden, wd[...], preferred_element_type=jnp.float32)
-            term[slot] = down.astype(jnp.bfloat16)
-            return 0
-
-        lax.fori_loop(0, 2, block, 0)
+            post[k * share : (k + 1) * share, :] = layer_norm(mixed[at, :], scale).astype(jnp.bfloat16)
+        up = jnp.dot(post[...], wu[...], preferred_element_type=jnp.float32)
+        hidden = jax.nn.gelu(up, approximate=True).astype(jnp.bfloat16)
+        for k in range(3):
+            cols = slice(k * (width // 3), (k + 1) * (width // 3))
+            down = jnp.dot(hidden, wd[:, cols], preferred_element_type=jnp.float32).astype(jnp.bfloat16)
+            for i, slot in enumerate(slots):
+                term[slot, :, cols] = down[i * share : (i + 1) * share]
 
     first, second = reduce_tensor(links, term, stage, share, width, feed_forward)
     at = pl.ds(pl.multiple_of(me * share, 32), share)
     out_ref[me, :, 0 : 2 * quarter] = (mixed[at, 0 : 2 * quarter] + first).astype(jnp.bfloat16)
-    out_ref[me, :, 2 * quarter :] = (mixed[at, 2 * quarter :] + second).astype(jnp.bfloat16)
-    gather_tensor(links, lambda slot, lo, hi: out_ref.at[slot, :, lo * quarter : hi * quarter])
+
+    def rest():
+        out_ref[me, :, 2 * quarter :] = (mixed[at, 2 * quarter :] + second()).astype(jnp.bfloat16)
+
+    gather_tensor(links, lambda slot, lo, hi: out_ref.at[slot, :, lo * quarter : hi * quarter], between=rest)
 
 
 def tail(o, w_out, tokens, gain, w_up, w_down):
@@ -619,22 +687,23 @@
     return pl.pallas_call(
         tail_kernel,
         out_shape=jax.ShapeDtypeStruct((8, share, cols), bf16),
-        in_specs=[FULL, anywhere, FULL, FULL, anywhere, anywhere],
+        in_specs=[FULL, anywhere, anywhere, FULL, anywhere, anywhere],
         out_specs=FULL,
         scratch_shapes=[
             pltpu.VMEM((8,) + o.shape, bf16),
             pltpu.VMEM((PAD, cols), jnp.float32),
-            pltpu.VMEM((share, cols), bf16),
+            pltpu.VMEM((2 * share, cols), bf16),
             pltpu.VMEM((8, share, cols), bf16),
             pltpu.VMEM((17, share, cols // 2), bf16),
+            pltpu.VMEM(tokens.shape, bf16),
             pltpu.VMEM(w_out.shape, bf16),
             pltpu.VMEM(w_up.shape, bf16),
             pltpu.VMEM(w_down.shape, bf16),
             pltpu.SemaphoreType.DMA((copies,)),
             pltpu.SemaphoreType.DMA((copies,)),
-            pltpu.SemaphoreType.DMA((3,)),
+            pltpu.SemaphoreType.DMA((4,)),
         ],
-        compiler_params=pltpu.CompilerParams(collective_id=1, has_side_effects=True, vmem_limit_bytes=48 * 2**20),
+        compiler_params=pltpu.CompilerParams(collective_id=1, has_side_effects=True, vmem_limit_bytes=54 * 2**20),
         name="tail",
     )(o, w_out, tokens, gain, w_up, w_down)
 
@@ -643,7 +712,7 @@
     rows, width = tokens.shape
     heads = w_qkv.shape[2] // HD
     o, w_out_all = attention(tokens, norm_gain, w_qkv, w_out)
-    out = tail(o, w_out_all.reshape(8, heads * HD, width), tokens, post_gain.reshape(1, width), w_up, w_down)
+    out = tail(o, w_out_all.reshape(8, heads * HD, width), tokens, post_gain.reshape(width // 128, 128), w_up, w_down)
     return out.reshape(PAD, width)[:rows]
 
 

time: 238 us -> 246 us (1.034)
  Pallas kernels: 229 us -> 239 us
  local copies, waits for them, and re-layouts: 5.99 us -> 3.12 us
    pallas_call x1, Pallas kernels: 175 us -> 185 us  [tail(): pl.pallas_call(tail_kernel, out_shape=jax.ShapeDtypeStruct((8, share, col...]
    unnamed x8 -> x0, local copies, waits for them, and re-layouts: 3.78 us -> none
where the time goes in v3:
time: 246 us; the launch traced here: 243 us
  Pallas kernels  239 us (97%)
  local copies, waits for them, and re-layouts  3.12 us (1%)
    pallas_call x1, Pallas kernels, tail(): pl.pallas_call(tail_kernel, out_shape=jax.ShapeDtypeStruct((8, share, col...  185 us
    pallas_call x1, Pallas kernels, attention(): pl.pallas_call(attend_kernel, out_shape=(jax.ShapeDtypeStruct((HD + 16, w...  52.2 us

profile of v3, /device:TPU:0, one launch (start us, length us, event | category | flops | bytes accessed | tf_op | source)
XLA Modules:
  0.0 242.6 jit_solution(14349893594132456047)
XLA Ops:
  0.0 52.2 %attend.1 = (f32[64,3072]{1,0:T(8,128)}, bf16[4,3,48,768]{3,2,1,0:T(8,128)(2,1)}, bf16[3,4,2,48,768]{4,3,2,1,0:T(8,128)(2,1)}, bf16[8,2,96,1536]{3,2,1,0:T(8,128)(2,1)}) custom-call(bf16[720,1536]{1,0:T(8,128)(2,1)} %tokens.3, f32[12,128]{1,0:T(8,128)} %bitcast.12, bf16[576,1536]{1,0:T(8,128)(2,1)} %bitcast.10, bf16[2,96,1536]{2,1,0:T(8,128)(2,1)} %bitcast.11), custom_call_target="tpu_custom_call" | custom-call | tf_op jit(solution)/shard_map/attend/pallas_call | solution.py:358
  52.2 2.1 settle.1.o_ref
  54.2 185.3 %tail.1 = bf16[8,96,1536]{2,1,0:T(8,128)(2,1)} custom-call(bf16[4,48,768]{2,1,0:T(8,128)(2,1)} %settle.1.o_ref, bf16[8,192,1536]{2,1,0:T(8,128)(2,1)} %bitcast.9, bf16[720,1536]{1,0:T(8,128)(2,1)} %tokens.3, f32[12,128]{1,0:T(8,128)} %bitcast.13, bf16[1536,768]{1,0:T(8,128)(2,1)} %w_up.1, bf16[768,1536]{1,0:T(8,128)(2,1)} %w_down.1), custom_call_target="tpu_custom_call" | custom-call | tf_op jit(solution)/shard_map/tail/pallas_call | solution.py:687
  239.5 3.1 %slice.4 = bf16[720,1536]{1,0:T(8,128)(2,1)} slice(bf16[768,1536]{1,0:T(8,128)(2,1)} %bitcast.8), slice={[0:720], [0:1536]} | slice | bytes 4423680 | tf_op jit(solution)/shard_map/slice | solution.py:716

commit v4 on v3

--- a/solution.py
+++ b/solution.py
@@ -78,8 +78,8 @@
 
 
 def attend_kernel(
-    tokens, gain, w_in, w_ref, acc, land_out, kvx_out, w_all,
-    tok, wq, w_own, normed, qkv, land, kvx, queries, keys, vals, probs, send, recv, local,
+    tokens, gain, w_in, w_ref, o_ref, totals, land_out, kvx_out, w_all,
+    tok, wq, w_own, normed, qkv, land, kvx, queries, keys, vals, probs, acc, send, recv, local,
 ):
     rows = tok.shape[0]
     width = queries.shape[1]
@@ -276,6 +276,8 @@
     probs[:, rows:PAD, :] = jnp.zeros((2, PAD - rows, WIDE), jnp.bfloat16)
     set_queries(0)
     sweep(rows, queries, keys, vals, acc, probs, early, late)
+    attended(acc, o_ref)
+    totals[...] = jnp.broadcast_to(acc[HD : HD + 1, :], totals.shape)
     for i in range(5):
         keep(i).wait()
     for pair in others:
@@ -283,22 +285,19 @@
     links.drain()
 
 
-def settle_kernel(rows, acc_in, land_ref, kvx_ref, o_ref, land, kvx, queries, keys, vals, probs, acc, local):
-    width = acc_in.shape[1]
-    total = acc_in[HD : HD + 1, :]
-    fits = jnp.where((total < LIMIT) & (total > FLOOR), 0.0, 1.0)
-    again = jnp.max(fits) > 0.5
-
-    def write(sums):
-        for i, d in enumerate(ORDER):
-            cols = slice(i * PAD, (i + 1) * PAD)
-            o_ref[d] = (sums[0:HD, cols] / sums[HD : HD + 1, cols]).astype(jnp.bfloat16)
-
-    @pl.when(jnp.logical_not(again))
-    def _():
-        write(acc_in)
-
-    @pl.when(again)
+def attended(sums, o_ref):
+    for i, d in enumerate(ORDER):
+        cols = slice(i * PAD, (i + 1) * PAD)
+        o_ref[d] = (sums[0:HD, cols] / sums[HD : HD + 1, cols]).astype(jnp.bfloat16)
+
+
+def settle_kernel(
+    rows, o_in, totals, land_ref, kvx_ref, o_out, o_new, land, kvx, queries, keys, vals, probs, acc, local
+):
+    width = totals.shape[1]
+    fits = jnp.where((totals[...] < LIMIT) & (totals[...] > FLOOR), 0.0, 1.0)
+
+    @pl.when(jnp.max(fits) > 0.5)
     def _():
         loads = [
             pltpu.make_async_copy(land_ref, land, local.at[0]),
@@ -339,7 +338,10 @@
             return 0
 
         lax.fori_loop(0, width // 256, chunk, 0)
-        write(acc)
+        attended(acc, o_new)
+        store = pltpu.make_async_copy(o_new, o_out, local.at[2])
+        store.start()
+        store.wait()
 
 
 def attention(tokens, gain, w_qkv, w_out):
@@ -355,16 +357,17 @@
     ]
     blocks = [pltpu.VMEM((4, 3, HD, PAD), bf16), pltpu.VMEM((3, 4, 2, HD, PAD), bf16)]
     anywhere = pl.BlockSpec(memory_space=pl.ANY)
-    acc, land, kvx, w_all = pl.pallas_call(
+    o, totals, land, kvx, w_all = pl.pallas_call(
         attend_kernel,
         out_shape=(
-            jax.ShapeDtypeStruct((HD + 16, width), jnp.float32),
+            jax.ShapeDtypeStruct((4, HD, PAD), bf16),
+            jax.ShapeDtypeStruct((8, width), jnp.float32),
             jax.ShapeDtypeStruct((4, 3, HD, PAD), bf16),
             jax.ShapeDtypeStruct((3, 4, 2, HD, PAD), bf16),
             jax.ShapeDtypeStruct((8, 2, half, cols), bf16),
         ),
         in_specs=[anywhere, FULL, anywhere, anywhere],
-        out_specs=(FULL, anywhere, anywhere, anywhere),
+        out_specs=(FULL, FULL, anywhere, anywhere, anywhere),
         scratch_shapes=[
             pltpu.VMEM(tokens.shape, bf16),
             pltpu.VMEM((3 * w_qkv.shape[2], features), bf16),
@@ -376,11 +379,12 @@
         + tables
         + [
             pltpu.VMEM((2, PAD, WIDE), bf16),
+            pltpu.VMEM((HD + 16, width), jnp.float32),
             pltpu.SemaphoreType.DMA((n,)),
             pltpu.SemaphoreType.DMA((n,)),
             pltpu.SemaphoreType.DMA((8,)),
         ],
-        compiler_params=pltpu.CompilerParams(collective_id=0, has_side_effects=True, vmem_limit_bytes=60 * 2**20),
+        compiler_params=pltpu.CompilerParams(collective_id=0, has_side_effects=True, vmem_limit_bytes=54 * 2**20),
         name="attend",
     )(
         tokens,
@@ -391,18 +395,20 @@
     o = pl.pallas_call(
         functools.partial(settle_kernel, rows),
         out_shape=jax.ShapeDtypeStruct((4, HD, PAD), bf16),
-        in_specs=[FULL, anywhere, anywhere],
-        out_specs=FULL,
-        scratch_shapes=blocks
+        in_specs=[anywhere, FULL, anywhere, anywhere],
+        out_specs=anywhere,
+        input_output_aliases={0: 0},
+        scratch_shapes=[pltpu.VMEM((4, HD, PAD), bf16)]
+        + blocks
         + tables
         + [
             pltpu.VMEM((PAD, 256), bf16),
             pltpu.VMEM((HD + 16, width), jnp.float32),
-            pltpu.SemaphoreType.DMA((2,)),
+            pltpu.SemaphoreType.DMA((3,)),
         ],
-        compiler_params=pltpu.CompilerParams(vmem_limit_bytes=60 * 2**20),
+        compiler_params=pltpu.CompilerParams(vmem_limit_bytes=61 * 2**20),
         name="settle",
-    )(acc, land, kvx)
+    )(o, totals, land, kvx)
     return o, w_all.reshape(16 * half, cols)
 
 
@@ -471,13 +477,13 @@
         return put(ref, ref, dz, dx)
 
     me = s(0, 0)
+    b_up = pass_on(me, 2, 4, 0, 1)
+    b_down = pass_on(me, 2, 4, 0, 3)
+    b_z = pass_on(me, 2, 4, 1, 0)
+    between()
     a_z = pass_on(me, 0, 2, 1, 0)
     a_up = pass_on(me, 0, 2, 0, 1)
     a_down = pass_on(me, 0, 2, 0, 3)
-    between()
-    b_up = pass_on(me, 2, 4, 0, 1)
-    b_down = pass_on(me, 2, 4, 0, 3)
-    b_z = pass_on(me, 2, 4, 1, 0)
     ready(0, 0)
     b_up.wait_recv()
     r2 = pass_on(s(0, 3), 2, 3, 0, 1)
@@ -590,16 +596,16 @@
     add_into(s(0, 1), 3, 4, got(1, 1, 2), got(13, 0, 1))
     add_into(s(0, 1), 2, 3, got(1, 0, 1))
     nb1 = put(q(s(0, 1), 2, 4), land(16, 2), 0, 1)
-    near[0, 3].wait_recv()
-    near[0, 1].wait_recv()
-    za.wait_recv()
-    first = val(s(0, 0), 0, 2) + got(9, 0, 2) + got(11, 0, 2) + got(14, 0, 2)
-
-    def second():
-        zb[0].wait_recv()
-        nb3.wait_recv()
-        nb1.wait_recv()
-        return val(s(0, 0), 2, 4) + got(3, 0, 2) + got(15, 0, 2) + got(16, 0, 2)
+    zb[0].wait_recv()
+    nb3.wait_recv()
+    nb1.wait_recv()
+    second = val(s(0, 0), 2, 4) + got(3, 0, 2) + got(15, 0, 2) + got(16, 0, 2)
+
+    def first():
+        near[0, 3].wait_recv()
+        near[0, 1].wait_recv()
+        za.wait_recv()
+        return val(s(0, 0), 0, 2) + got(9, 0, 2) + got(11, 0, 2) + got(14, 0, 2)
 
     return first, second
 
@@ -670,10 +676,10 @@
 
     first, second = reduce_tensor(links, term, stage, share, width, feed_forward)
     at = pl.ds(pl.multiple_of(me * share, 32), share)
-    out_ref[me, :, 0 : 2 * quarter] = (mixed[at, 0 : 2 * quarter] + first).astype(jnp.bfloat16)
+    out_ref[me, :, 2 * quarter :] = (mixed[at, 2 * quarter :] + second).astype(jnp.bfloat16)
 
     def rest():
-        out_ref[me, :, 2 * quarter :] = (mixed[at, 2 * quarter :] + second()).astype(jnp.bfloat16)
+        out_ref[me, :, 0 : 2 * quarter] = (mixed[at, 0 : 2 * quarter] + first()).astype(jnp.bfloat16)
 
     gather_tensor(links, lambda slot, lo, hi: out_ref.at[slot, :, lo * quarter : hi * quarter], between=rest)
 
@@ -703,7 +709,7 @@
             pltpu.SemaphoreType.DMA((copies,)),
             pltpu.SemaphoreType.DMA((4,)),
         ],
-        compiler_params=pltpu.CompilerParams(collective_id=1, has_side_effects=True, vmem_limit_bytes=54 * 2**20),
+        compiler_params=pltpu.CompilerParams(collective_id=1, has_side_effects=True, vmem_limit_bytes=48 * 2**20),
         name="tail",
     )(o, w_out, tokens, gain, w_up, w_down)
 

time: 246 us -> 238 us (0.967)
  Pallas kernels: 239 us -> 235 us
    pallas_call x1, Pallas kernels: 185 us -> 63.1 us  [tail(): pl.pallas_call(tail_kernel, out_shape=jax.ShapeDtypeStruct((8, share, col...]
    pallas_call x1, Pallas kernels: 2.06 us -> 119 us  [attention(): pl.pallas_call(functools.partial(settle_kernel, rows), out_shape=jax.Shap...]
where the time goes in v4:
time: 238 us; the launch traced here: 237 us
  Pallas kernels  235 us (99%)
  local copies, waits for them, and re-layouts  2.47 us (1%)
    pallas_call x1, Pallas kernels, attention(): pl.pallas_call(functools.partial(settle_kernel, rows), out_shape=jax.Shap...  119 us
    pallas_call x1, Pallas kernels, tail(): pl.pallas_call(tail_kernel, out_shape=jax.ShapeDtypeStruct((8, share, col...  63.1 us
    pallas_call x1, Pallas kernels, attention(): pl.pallas_call(attend_kernel, out_shape=(jax.ShapeDtypeStruct((4, HD, PAD...  52.1 us

profile of v4, /device:TPU:0, one launch (start us, length us, event | category | flops | bytes accessed | tf_op | source)
XLA Modules:
  0.0 237.1 jit_solution(17583384497245256484)
XLA Ops:
  0.0 52.1 %attend.1 = (bf16[4,48,768]{2,1,0:T(8,128)(2,1)}, f32[8,3072]{1,0:T(8,128)}, bf16[4,3,48,768]{3,2,1,0:T(8,128)(2,1)}, bf16[3,4,2,48,768]{4,3,2,1,0:T(8,128)(2,1)}, bf16[8,2,96,1536]{3,2,1,0:T(8,128)(2,1)}) custom-call(bf16[720,1536]{1,0:T(8,128)(2,1)} %tokens.3, f32[12,128]{1,0:T(8,128)} %bitcast.13, bf16[576,1536]{1,0:T(8,128)(2,1)} %bitcast.11, ...), custom_call_target="tpu_custom_call" | custom-call | tf_op jit(solution)/shard_map/attend/pallas_call | solution.py:360
  52.1 0.0 copy-start
  52.1 0.0 copy-start.2
  52.1 119.3 %settle.1.o_ref = bf16[4,48,768]{2,1,0:T(8,128)(2,1)} custom-call(bf16[4,48,768]{2,1,0:T(8,128)(2,1)} %get-tuple-element.10.o_in, f32[8,3072]{1,0:T(8,128)} %get-tuple-element.11.totals, bf16[4,3,48,768]{3,2,1,0:T(8,128)(2,1)} %get-tuple-element.12.land_ref, bf16[3,4,2,48,768]{4,3,2,1,0:T(8,128)(2,1)} %get-tuple-element.13.kvx_ref), custom_call_target="tpu_custom_call", output_to_operand_aliasing={{}: (0, {})} | custom-call | tf_op jit(solution)/shard_map/settle/pallas_call | solution.py:395
  171.4 0.0 copy-done
  171.4 0.0 copy-done.2
  171.5 0.0 copy-start.1
  171.5 1.0 copy-done.1
  172.4 63.1 %tail.1 = bf16[8,96,1536]{2,1,0:T(8,128)(2,1)S(1)} custom-call(bf16[4,48,768]{2,1,0:T(8,128)(2,1)S(1)} %copy-done.1, bf16[8,192,1536]{2,1,0:T(8,128)(2,1)} %bitcast.10, bf16[720,1536]{1,0:T(8,128)(2,1)S(1)} %copy-done, f32[12,128]{1,0:T(8,128)S(1)} %bitcast.9, bf16[1536,768]{1,0:T(8,128)(2,1)} %w_up.1, bf16[768,1536]{1,0:T(8,128)(2,1)} %w_down.1), custom_call_target="tpu_custom_call" | custom-call | tf_op jit(solution)/shard_map/tail/pallas_call | solution.py:693
  235.6 1.5 slice.4
Async XLA Ops:
  52.1 119.4 %copy-start = (bf16[720,1536]{1,0:T(8,128)(2,1)S(1)}, bf16[720,1536]{1,0:T(8,128)(2,1)}, u32[]{:S(2)}) copy-start(bf16[720,1536]{1,0:T(8,128)(2,1)} %tokens.3) | copy-start | bytes 6635524
  52.1 119.4 %copy-start.2 = (f32[1536]{0:T(1024)S(1)}, f32[1536]{0:T(1024)}, u32[]{:S(2)}) copy-start(f32[1536]{0:T(1024)} %param.11) | copy-start | bytes 18436
  171.5 1.0 copy-start.1

commit v5 on v4

--- a/solution.py
+++ b/solution.py
@@ -66,15 +66,21 @@
 ORDER = (0, 1, 3, 2)
 
 
-def load_block(rows, kv, b, keys, vals):
+def load_keys(src, b, keys):
+    one = (lax.broadcasted_iota(jnp.int32, (16, PAD), 0) == 0).astype(jnp.float32).astype(jnp.bfloat16)
+    keys[b] = jnp.concatenate([src[...], one, jnp.zeros((64, PAD), jnp.bfloat16)], axis=0).T
+
+
+def load_values(rows, src, b, vals):
     lane = lax.broadcasted_iota(jnp.int32, (16, PAD), 1)
     sub = lax.broadcasted_iota(jnp.int32, (16, PAD), 0)
-    count = ((sub == 0) & (lane < rows)).astype(jnp.float32).astype(jnp.bfloat16)
-    shift = (sub == 0).astype(jnp.float32).astype(jnp.bfloat16)
-    zeros = jnp.zeros((64, PAD), jnp.bfloat16)
-    keys[b] = jnp.concatenate([kv[0], shift, zeros], axis=0).T
-    vals[b, 0:HD] = kv[1]
-    vals[b, HD : HD + 16] = count
+    vals[b, 0:HD] = src[...]
+    vals[b, HD : HD + 16] = ((sub == 0) & (lane < rows)).astype(jnp.float32).astype(jnp.bfloat16)
+
+
+def load_block(rows, kv, b, keys, vals):
+    load_keys(kv.at[0], b, keys)
+    load_values(rows, kv.at[1], b, vals)
 
 
 def attend_kernel(
@@ -136,8 +142,14 @@
     pl.semaphore_wait(barrier, 8)
 
     by_y = {}
-    for d in (1, 3, 2):
-        by_y[d] = links.start(lambda d=d: (qkv.at[:, lax.rem(y + d, 4)], land.at[d], on_seq(0, d, 0)))
+
+    def send_y(d, lo, hi):
+        by_y[d, lo] = links.start(
+            lambda: (qkv.at[lo:hi, lax.rem(y + d, 4)], land.at[d, lo:hi], on_seq(0, d, 0))
+        )
+
+    for d, lo, hi in ((1, 0, 2), (3, 0, 2), (1, 2, 3), (3, 2, 3), (2, 0, 2), (2, 2, 3)):
+        send_y(d, lo, hi)
     to_core, to_far, far_core, more = {}, {}, {}, {}
     to_core[0] = links.start(lambda: (qkv.at[1:3, y], kvx.at[0, 0], on_seq(0, 0, 1)))
     to_far[0] = links.start(lambda: (qkv.at[1:3, y], kvx.at[1, 0], on_seq(1, 0, 0)))
@@ -180,12 +192,16 @@
         queries[HD : HD + 16, cols] = shift.astype(jnp.bfloat16)
 
     def arrive(i):
+        by_y[ORDER[i], 0].wait_recv()
+        load_keys(land.at[ORDER[i], 1], i, keys)
+        set_queries(i)
+
+    def arrive_values(i):
         d = ORDER[i]
-        by_y[d].wait_recv()
+        by_y[d, 2].wait_recv()
         to_core[d] = links.start(lambda: (land.at[d, 1:3], kvx.at[0, d], on_seq(0, 0, 1)))
         to_far[d] = links.start(lambda: (land.at[d, 1:3], kvx.at[1, d], on_seq(1, 0, 0)))
-        load_block(rows, land.at[d, 1:3], i, keys, vals)
-        set_queries(i)
+        load_values(rows, land.at[d, 2], i, vals)
 
     def take(block):
         group, d = block // 4, ORDER[block % 4]
@@ -233,10 +249,11 @@
 
     early = {
         1: both((arrive, 1), (arrive, 2)),
+        2: both((arrive_values, 1), (arrive_values, 2)),
         9: both((take, 4),),
         12: both((take, 5),),
         15: both((take, 6),),
-        18: both((arrive, 3), (w_first,), (store, 1)),
+        18: both((arrive, 3), (arrive_values, 3), (w_first,), (store, 1)),
         21: both((take, 7), (store, 2)),
         32: both((take, 8),),
     }
@@ -526,45 +543,49 @@
 GATHER_COPIES = 18
 
 
+def cuts(cols):
+    return [cols // 12 * k for k in (0, 4, 7, 9, 12)]
+
+
 def reduce_tensor(links, term, stage, rows, cols, make):
-    quarter = cols // 4
+    at = cuts(cols)
     s = links.slot
     put = links.put
 
     def q(slot, lo, hi):
-        return term.at[slot, :, lo * quarter : hi * quarter]
+        return term.at[slot, :, at[lo] : at[hi]]
 
     def val(slot, lo, hi):
-        return term[slot, :, lo * quarter : hi * quarter].astype(jnp.float32)
-
-    def land(i, n):
-        return stage.at[i, :, 0 : n * quarter]
-
-    def got(i, lo, hi):
-        return stage[i, :, lo * quarter : hi * quarter].astype(jnp.float32)
+        return term[slot, :, at[lo] : at[hi]].astype(jnp.float32)
+
+    def land(i, lo, hi):
+        return stage.at[i, :, 0 : at[hi] - at[lo]]
+
+    def got(i, base, lo, hi):
+        return stage[i, :, at[lo] - at[base] : at[hi] - at[base]].astype(jnp.float32)
 
     def add_into(slot, lo, hi, *parts):
         total = val(slot, lo, hi)
         for part in parts:
             total = total + part
-        term[slot, :, lo * quarter : hi * quarter] = total.astype(jnp.bfloat16)
+        term[slot, :, at[lo] : at[hi]] = total.astype(jnp.bfloat16)
 
     zb, fa, near = {}, {}, {}
 
     def cross(i, dx):
-        zb[dx] = put(q(s(1, dx), 2, 4), land(i, 2), 1, 0)
+        zb[dx] = put(q(s(1, dx), 2, 4), land(i, 2, 4), 1, 0)
 
     def far(j, dz):
-        fa[dz, 0] = put(q(s(dz, 2), 0, 1), land(4 + j, 1), 0, 3)
-        fa[dz, 1] = put(q(s(dz, 2), 1, 2), land(6 + j, 1), 0, 1)
+        fa[dz, 0] = put(q(s(dz, 2), 0, 1), land(4 + j, 0, 1), 0, 3)
+        fa[dz, 1] = put(q(s(dz, 2), 1, 2), land(6 + j, 1, 2), 0, 1)
 
     def relay(j, dz):
         fa[dz, 0].wait_recv()
-        add_into(s(dz, 3), 0, 1, got(4 + j, 0, 1))
-        near[dz, 3] = put(q(s(dz, 3), 0, 2), land(8 + j, 2), 0, 3)
+        add_into(s(dz, 3), 0, 1, got(4 + j, 0, 0, 1))
+        near[dz, 3] = put(q(s(dz, 3), 0, 2), land(8 + j, 0, 2), 0, 3)
         fa[dz, 1].wait_recv()
-        add_into(s(dz, 1), 1, 2, got(6 + j, 0, 1))
-        near[dz, 1] = put(q(s(dz, 1), 0, 2), land(10 + j, 2), 0, 1)
+        add_into(s(dz, 1), 1, 2, got(6 + j, 1, 1, 2))
+        near[dz, 1] = put(q(s(dz, 1), 0, 2), land(10 + j, 0, 2), 0, 1)
 
     make((1, 2), (0, 2))
     cross(0, 2)
@@ -577,35 +598,35 @@
     make((0, 1), (0, 3))
     relay(1, 0)
     zb[2].wait_recv()
-    add_into(s(0, 2), 2, 4, got(0, 0, 2))
-    fb0 = put(q(s(0, 2), 2, 3), land(12, 1), 0, 3)
-    fb1 = put(q(s(0, 2), 3, 4), land(13, 1), 0, 1)
+    add_into(s(0, 2), 2, 4, got(0, 2, 2, 4))
+    fb0 = put(q(s(0, 2), 2, 3), land(12, 2, 3), 0, 3)
+    fb1 = put(q(s(0, 2), 3, 4), land(13, 3, 4), 0, 1)
     make((1, 0), (0, 0))
     cross(3, 0)
     zb[1].wait_recv()
     zb[3].wait_recv()
     near[1, 3].wait_recv()
     near[1, 1].wait_recv()
-    add_into(s(1, 0), 0, 2, got(8, 0, 2), got(10, 0, 2))
-    za = put(q(s(1, 0), 0, 2), land(14, 2), 1, 0)
+    add_into(s(1, 0), 0, 2, got(8, 0, 0, 2), got(10, 0, 0, 2))
+    za = put(q(s(1, 0), 0, 2), land(14, 0, 2), 1, 0)
     fb0.wait_recv()
-    add_into(s(0, 3), 2, 3, got(2, 0, 1), got(12, 0, 1))
-    add_into(s(0, 3), 3, 4, got(2, 1, 2))
-    nb3 = put(q(s(0, 3), 2, 4), land(15, 2), 0, 3)
+    add_into(s(0, 3), 2, 3, got(2, 2, 2, 3), got(12, 2, 2, 3))
+    add_into(s(0, 3), 3, 4, got(2, 2, 3, 4))
+    nb3 = put(q(s(0, 3), 2, 4), land(15, 2, 4), 0, 3)
     fb1.wait_recv()
-    add_into(s(0, 1), 3, 4, got(1, 1, 2), got(13, 0, 1))
-    add_into(s(0, 1), 2, 3, got(1, 0, 1))
-    nb1 = put(q(s(0, 1), 2, 4), land(16, 2), 0, 1)
+    add_into(s(0, 1), 3, 4, got(1, 2, 3, 4), got(13, 3, 3, 4))
+    add_into(s(0, 1), 2, 3, got(1, 2, 2, 3))
+    nb1 = put(q(s(0, 1), 2, 4), land(16, 2, 4), 0, 1)
     zb[0].wait_recv()
     nb3.wait_recv()
     nb1.wait_recv()
-    second = val(s(0, 0), 2, 4) + got(3, 0, 2) + got(15, 0, 2) + got(16, 0, 2)
+    second = val(s(0, 0), 2, 4) + got(3, 2, 2, 4) + got(15, 2, 2, 4) + got(16, 2, 2, 4)
 
     def first():
         near[0, 3].wait_recv()
         near[0, 1].wait_recv()
         za.wait_recv()
-        return val(s(0, 0), 0, 2) + got(9, 0, 2) + got(11, 0, 2) + got(14, 0, 2)
+        return val(s(0, 0), 0, 2) + got(9, 0, 0, 2) + got(11, 0, 0, 2) + got(14, 0, 0, 2)
 
     return first, second
 
@@ -617,7 +638,7 @@
     seq, me = links.seq, links.me
     y = lax.rem(seq // 2, 4)
     share, width = out_ref.shape[1], out_ref.shape[2]
-    quarter = width // 4
+    cut = cuts(width)
     rows = tok.shape[0]
     loads = [
         pltpu.make_async_copy(src, dst, local.at[i])
@@ -676,12 +697,12 @@
 
     first, second = reduce_tensor(links, term, stage, share, width, feed_forward)
     at = pl.ds(pl.multiple_of(me * share, 32), share)
-    out_ref[me, :, 2 * quarter :] = (mixed[at, 2 * quarter :] + second).astype(jnp.bfloat16)
+    out_ref[me, :, cut[2] :] = (mixed[at, cut[2] :] + second).astype(jnp.bfloat16)
 
     def rest():
-        out_ref[me, :, 0 : 2 * quarter] = (mixed[at, 0 : 2 * quarter] + first()).astype(jnp.bfloat16)
-
-    gather_tensor(links, lambda slot, lo, hi: out_ref.at[slot, :, lo * quarter : hi * quarter], between=rest)
+        out_ref[me, :, 0 : cut[2]] = (mixed[at, 0 : cut[2]] + first()).astype(jnp.bfloat16)
+
+    gather_tensor(links, lambda slot, lo, hi: out_ref.at[slot, :, cut[lo] : cut[hi]], between=rest)
 
 
 def tail(o, w_out, tokens, gain, w_up, w_down):
@@ -700,7 +721,7 @@
             pltpu.VMEM((PAD, cols), jnp.float32),
             pltpu.VMEM((2 * share, cols), bf16),
             pltpu.VMEM((8, share, cols), bf16),
-            pltpu.VMEM((17, share, cols // 2), bf16),
+            pltpu.VMEM((17, share, cols // 12 * 7), bf16),
             pltpu.VMEM(tokens.shape, bf16),
             pltpu.VMEM(w_out.shape, bf16),
             pltpu.VMEM(w_up.shape, bf16),

time: 238 us -> 239 us (level)
    pallas_call x1, Pallas kernels: 63.1 us -> 185 us  [tail(): pl.pallas_call(tail_kernel, out_shape=jax.ShapeDtypeStruct((8, share, col...]
    pallas_call x1, Pallas kernels: 119 us -> 1.21 us  [attention(): pl.pallas_call(functools.partial(settle_kernel, rows), out_shape=jax.Shap...]
where the time goes in v5:
time: 239 us; the launch traced here: 240 us
  Pallas kernels  237 us (99%)
  local copies, waits for them, and re-layouts  2.9 us (1%)
    pallas_call x1, Pallas kernels, tail(): pl.pallas_call(tail_kernel, out_shape=jax.ShapeDtypeStruct((8, share, col...  185 us
    pallas_call x1, Pallas kernels, attention(): pl.pallas_call(attend_kernel, out_shape=(jax.ShapeDtypeStruct((4, HD, PAD...  50.7 us

profile of v5, /device:TPU:0, one launch (start us, length us, event | category | flops | bytes accessed | tf_op | source)
XLA Modules:
  0.0 239.5 jit_solution(6073892818860818776)
XLA Ops:
  0.0 50.7 %attend.1 = (bf16[4,48,768]{2,1,0:T(8,128)(2,1)}, f32[8,3072]{1,0:T(8,128)}, bf16[4,3,48,768]{3,2,1,0:T(8,128)(2,1)}, bf16[3,4,2,48,768]{4,3,2,1,0:T(8,128)(2,1)}, bf16[8,2,96,1536]{3,2,1,0:T(8,128)(2,1)}) custom-call(bf16[720,1536]{1,0:T(8,128)(2,1)} %tokens.3, f32[12,128]{1,0:T(8,128)} %bitcast.13, bf16[576,1536]{1,0:T(8,128)(2,1)} %bitcast.11, ...), custom_call_target="tpu_custom_call" | custom-call | tf_op jit(solution)/shard_map/attend/pallas_call | solution.py:377
  50.7 0.0 copy-start
  50.7 0.0 copy-start.2
  50.7 1.2 settle.1.o_ref
  51.9 0.4 copy-done
  52.4 0.0 copy-done.2
  52.4 0.0 copy-start.1
  52.4 1.0 copy-done.1
  53.3 184.7 %tail.1 = bf16[8,96,1536]{2,1,0:T(8,128)(2,1)S(1)} custom-call(bf16[4,48,768]{2,1,0:T(8,128)(2,1)S(1)} %copy-done.1, bf16[8,192,1536]{2,1,0:T(8,128)(2,1)} %bitcast.10, bf16[720,1536]{1,0:T(8,128)(2,1)S(1)} %copy-done, f32[12,128]{1,0:T(8,128)S(1)} %bitcast.9, bf16[1536,768]{1,0:T(8,128)(2,1)} %w_up.1, bf16[768,1536]{1,0:T(8,128)(2,1)} %w_down.1), custom_call_target="tpu_custom_call" | custom-call | tf_op jit(solution)/shard_map/tail/pallas_call | solution.py:714
  238.0 1.5 slice.4
Async XLA Ops:
  50.7 1.7 copy-start
  50.7 1.7 copy-start.2
  52.4 1.0 copy-start.1

commit v6 on v5

--- a/solution.py
+++ b/solution.py
@@ -496,9 +496,9 @@
     me = s(0, 0)
     b_up = pass_on(me, 2, 4, 0, 1)
     b_down = pass_on(me, 2, 4, 0, 3)
-    b_z = pass_on(me, 2, 4, 1, 0)
     between()
     a_z = pass_on(me, 0, 2, 1, 0)
+    b_z = pass_on(me, 2, 4, 1, 0)
     a_up = pass_on(me, 0, 2, 0, 1)
     a_down = pass_on(me, 0, 2, 0, 3)
     ready(0, 0)
@@ -544,7 +544,7 @@
 
 
 def cuts(cols):
-    return [cols // 12 * k for k in (0, 4, 7, 9, 12)]
+    return [cols // 12 * k for k in (0, 3, 6, 9, 12)]
 
 
 def reduce_tensor(links, term, stage, rows, cols, make):
@@ -721,7 +721,7 @@
             pltpu.VMEM((PAD, cols), jnp.float32),
             pltpu.VMEM((2 * share, cols), bf16),
             pltpu.VMEM((8, share, cols), bf16),
-            pltpu.VMEM((17, share, cols // 12 * 7), bf16),
+            pltpu.VMEM((17, share, cols // 2), bf16),
             pltpu.VMEM(tokens.shape, bf16),
             pltpu.VMEM(w_out.shape, bf16),
             pltpu.VMEM(w_up.shape, bf16),

time: 239 us -> 237 us (level)
  Pallas kernels: 237 us -> 234 us
    pallas_call x1, Pallas kernels: 185 us -> 182 us  [tail(): pl.pallas_call(tail_kernel, out_shape=jax.ShapeDtypeStruct((8, share, col...]
where the time goes in v6:
time: 237 us
  Pallas kernels  234 us (99%)
  local copies, waits for them, and re-layouts  2.9 us (1%)
    pallas_call x1, Pallas kernels, tail(): pl.pallas_call(tail_kernel, out_shape=jax.ShapeDtypeStruct((8, share, col...  182 us
    pallas_call x1, Pallas kernels, attention(): pl.pallas_call(attend_kernel, out_shape=(jax.ShapeDtypeStruct((4, HD, PAD...  50.7 us

profile of v6, /device:TPU:0, one launch (start us, length us, event | category | flops | bytes accessed | tf_op | source)
XLA Modules:
  0.0 236.8 jit_solution(17586260607207168542)
XLA Ops:
  0.0 50.7 %attend.1 = (bf16[4,48,768]{2,1,0:T(8,128)(2,1)}, f32[8,3072]{1,0:T(8,128)}, bf16[4,3,48,768]{3,2,1,0:T(8,128)(2,1)}, bf16[3,4,2,48,768]{4,3,2,1,0:T(8,128)(2,1)}, bf16[8,2,96,1536]{3,2,1,0:T(8,128)(2,1)}) custom-call(bf16[720,1536]{1,0:T(8,128)(2,1)} %tokens.3, f32[12,128]{1,0:T(8,128)} %bitcast.13, bf16[576,1536]{1,0:T(8,128)(2,1)} %bitcast.11, ...), custom_call_target="tpu_custom_call" | custom-call | tf_op jit(solution)/shard_map/attend/pallas_call | solution.py:377
  50.7 0.0 copy-start
  50.7 0.0 copy-start.2
  50.7 1.2 settle.1.o_ref
  51.9 0.4 copy-done
  52.4 0.0 copy-done.2
  52.4 0.0 copy-start.1
  52.4 1.0 copy-done.1
  53.3 182.0 %tail.1 = bf16[8,96,1536]{2,1,0:T(8,128)(2,1)S(1)} custom-call(bf16[4,48,768]{2,1,0:T(8,128)(2,1)S(1)} %copy-done.1, bf16[8,192,1536]{2,1,0:T(8,128)(2,1)} %bitcast.10, bf16[720,1536]{1,0:T(8,128)(2,1)S(1)} %copy-done, f32[12,128]{1,0:T(8,128)S(1)} %bitcast.9, bf16[1536,768]{1,0:T(8,128)(2,1)} %w_up.1, bf16[768,1536]{1,0:T(8,128)(2,1)} %w_down.1), custom_call_target="tpu_custom_call" | custom-call | tf_op jit(solution)/shard_map/tail/pallas_call | solution.py:714
  235.3 1.5 slice.4
Async XLA Ops:
  50.7 1.7 copy-start
  50.7 1.7 copy-start.2
  52.4 1.0 copy-start.1
